TPU v7x, 256 devices: a 4x2x16 block of a 4x16x16 slice. The times are simulated.
256 devices in a mesh: groups: 2 (over y), tx: 16 (over z), ty: 4 (over x), ka: 2 (over core).
Axes of the slice: x: 4, y: 2, z: 16, core: 2. Of those that a mesh axis runs over, the one named last changes fastest.
The devices are a block of a 4x16x16 slice.
Arguments:
- mask_raster: float32 [8192, 1024], P(('groups', 'tx'), 'ty'), parts along dimension 0, may hold values from 0 to 1
- frag_rows: int32 [32, 4, 512], P(('groups', 'tx'), 'ty'), parts along dimension 0, may hold values from 8 to 215
- frag_cols: int32 [32, 4, 512], P(('groups', 'tx'), 'ty'), parts along dimension 0, may hold values from 8 to 215
- frag_length: int32 [32, 4, 512], P(('groups', 'tx'), 'ty'), parts along dimension 0, may hold values from 4 to 32
- frag_orient: int32 [32, 4, 512], P(('groups', 'tx'), 'ty'), parts along dimension 0, may hold values from 0 to 1
- frag_moves: int32 [32, 4, 2, 512], P(('groups', 'tx'), 'ty'), parts along dimension 0, may hold values from -4 to 4
- site_rows: int32 [32, 4, 2048], P(('groups', 'tx'), 'ty'), parts along dimension 0, may hold values from 1 to 254
- site_cols: int32 [32, 4, 2048], P(('groups', 'tx'), 'ty'), parts along dimension 0, may hold values from 1 to 254
- spectra: float32 [16, 2, 128, 128], P('ka'), may hold values from -24 to 24
- weights: float32 [16], P('ka'), may hold values from 0.05 to 1
- tolerance: int32 [2], replicated, may hold values from 1 to 16
Outputs:
- intensity: float32 [8192, 1024], P(('groups', 'tx'), 'ty'), parts along dimension 0
- corrected_mask: float32 [8192, 1024], P(('groups', 'tx'), 'ty'), parts along dimension 0
- edge_errors: float32 [32, 4, 2, 2048], P(('groups', 'tx'), 'ty'), parts along dimension 0
- peak_error: float32 [4], P('groups'), parts along dimension 0
- converged_share: float32 [4], P('groups'), parts along dimension 0
There are 2 independent parts, one for each index of `groups`. A program takes and returns all parts, laid end to end along the dimension named above; an argument that names none is the same for every part. Nothing has to cross between parts.
All inputs are finite; a program needn't handle non-finite values.
Results may differ from a plain program's by a relative error of at most 0.0003.
Values sent between devices are 32-bit elements; how exact they have to be, the bound alone decides.
A program may use at most 64 MiB of HBM per device.

v0:
```python
import functools
import math

import jax
import jax.numpy as jnp
import numpy as np
from jax import lax
from jax.experimental import pallas as pl
from jax.experimental.pallas import tpu as pltpu
from jax.sharding import PartitionSpec as P

HALO = 128
BAND = 128
ITERS = 2
LEVEL = 0.4
SLOPE_FLOOR = 0.05
SHARPNESS = 8.0
HIGHEST = lax.Precision.HIGHEST
MESH = pl.DeviceIdType.MESH
SIN_AT = 72
PACKED = 136


def bf16_pieces(x, count):
    pieces = []
    for _ in range(count):
        pieces.append(x.astype(jnp.bfloat16))
        x = x - pieces[-1].astype(jnp.float32)
    return pieces


def host_pieces(x):
    pieces = []
    for _ in range(3):
        pieces.append(x.astype(jnp.bfloat16))
        x = x - pieces[-1].astype(np.float64)
    return pieces


def tables(tile):
    ext = tile + 2 * HALO
    half = tile // 2
    theta = 2.0 * math.pi / ext
    inside = np.arange(ext) - (ext - 1) / 2
    low = BAND // 2
    rows = np.zeros((PACKED, ext))
    rows[: low + 1] = np.cos(theta * np.outer(np.arange(low + 1), inside))
    rows[SIN_AT : SIN_AT + low] = np.sin(theta * np.outer(np.arange(1, low + 1), inside))
    freq = np.arange(BAND) - low
    turns = theta * np.outer(inside, freq)
    cols = np.concatenate([np.cos(turns), np.sin(turns)], axis=1)
    expand = np.zeros((2 * BAND, PACKED))
    for u, f in enumerate(freq):
        expand[u, abs(f)] = 1.0
        if f != 0:
            expand[BAND + u, SIN_AT + abs(f) - 1] = np.sign(f)
    out = theta * np.outer(freq, np.arange(half) + 0.5)
    basis = np.concatenate([np.cos(out), np.sin(out)], axis=1)
    hi, mid, lo = host_pieces(basis)
    first = np.stack([np.concatenate(b, axis=0) for b in ((hi, hi), (mid, mid), (lo, hi))])
    second = np.ascontiguousarray(first.swapaxes(1, 2))
    flip = np.eye(half)[::-1]
    f32 = np.float32
    return rows.astype(f32), cols.astype(f32), expand.astype(f32), first, second, flip.astype(f32)


def exact(left, right):
    return jnp.dot(left, right, precision=HIGHEST, preferred_element_type=jnp.float32)


def dot(left, right):
    return jnp.dot(left, right, preferred_element_type=jnp.float32)


def halo_kernel(
    mask, rows_at, cols_at, lengths, orients, moves, spectra, weights, row_dft, col_dft, expand,
    new_mask, spec_re, spec_im, other_spectra, other_weights,
    current, above, below, packed, left, right, my_weights, send_sem, recv_sem,
):
    tx, ty, ka = lax.axis_index("tx"), lax.axis_index("ty"), lax.axis_index("ka")
    tile = mask.shape[0]
    ext = tile + 2 * HALO
    has_up, has_down = tx > 0, tx < lax.axis_size("tx") - 1
    has_left, has_right = ty > 0, ty < lax.axis_size("ty") - 1
    barrier = pltpu.get_barrier_semaphore()
    near = ((has_up, "tx", tx - 1), (has_down, "tx", tx + 1), (has_left, "ty", ty - 1), (has_right, "ty", ty + 1))
    for there, axis, index in near:
        @pl.when(there)
        def _():
            pl.semaphore_signal(barrier, inc=1, device_id={axis: index}, device_id_type=MESH)
    pl.semaphore_signal(barrier, inc=1, device_id={"ka": 1 - ka}, device_id_type=MESH)

    for k in range(my_weights.shape[0]):
        my_weights[pl.ds(k, 1), :] = jnp.full((1, my_weights.shape[1]), weights[k], jnp.float32)
    position = lax.broadcasted_iota(jnp.int32, (tile, rows_at.shape[2]), 0)
    row, col, length = rows_at[0], cols_at[0], lengths[0]
    along = orients[0] == 0
    steps = [mask[...]]
    for t in range(ITERS):
        move = moves[0, 0, t : t + 1, :]
        lower, upper = jnp.minimum(move, 0), jnp.maximum(move, 0)
        row_low = jnp.where(along, row, row + lower)
        row_high = jnp.where(along, row + length, row + upper)
        col_low = jnp.where(along, col + lower, col)
        col_high = jnp.where(along, col + upper, col + length)
        sign = jnp.where(move > 0, 1.0, 0.0) - jnp.where(move < 0, 1.0, 0.0)
        in_rows = jnp.where((position >= row_low) & (position < row_high), sign, 0.0)
        in_cols = jnp.where((position >= col_low) & (position < col_high), 1.0, 0.0)
        strips = lax.dot_general(
            in_rows.astype(jnp.bfloat16), in_cols.astype(jnp.bfloat16), (((1,), (1,)), ((), ())),
            preferred_element_type=jnp.float32,
        )
        steps.append(jnp.clip(steps[-1] + strips, 0.0, 1.0))
    new_mask[...] = steps[2]
    current[...] = jnp.where(ka == 0, steps[1], steps[2])

    count = sum(there.astype(jnp.int32) for there, _, _ in near) + 1
    pl.semaphore_wait(barrier, count)

    def hop(source, target, number, device):
        return pltpu.make_async_remote_copy(
            src_ref=source, dst_ref=target, send_sem=send_sem.at[number], recv_sem=recv_sem.at[number],
            device_id=device, device_id_type=MESH,
        )

    half = tile // 2
    to_up = hop(current.at[pl.ds(0, half)], below, 0, {"tx": tx - 1})
    to_down = hop(current.at[pl.ds(half, half)], above, 1, {"tx": tx + 1})
    to_left = hop(packed.at[:, pl.ds(0, half)], right, 2, {"ty": ty - 1})
    to_right = hop(packed.at[:, pl.ds(half, half)], left, 3, {"ty": ty + 1})
    swap_weights = hop(my_weights, other_weights, 4, {"ka": 1 - ka})
    swap_spectra = hop(spectra, other_spectra, 5, {"ka": 1 - ka})
    pl.when(has_up)(to_up.start)
    pl.when(has_down)(to_down.start)
    swap_spectra.start()
    swap_weights.start()

    part = exact(row_dft[:, HALO : HALO + tile], current[...])

    def arrived(there, copy, buffer):
        pl.when(there)(copy.wait_recv)

        @pl.when(jnp.logical_not(there))
        def _():
            buffer[...] = jnp.zeros_like(buffer)

    arrived(has_up, to_down, above)
    arrived(has_down, to_up, below)
    part = part + exact(row_dft[:, :HALO], above[...]) + exact(row_dft[:, HALO + tile :], below[...])
    packed[...] = part
    pl.when(has_left)(to_left.start)
    pl.when(has_right)(to_right.start)
    sums = exact(part, col_dft[HALO : HALO + tile, :])
    arrived(has_left, to_right, left)
    arrived(has_right, to_left, right)
    sums = sums + exact(left[...], col_dft[:HALO, :]) + exact(right[...], col_dft[HALO + tile :, :])
    full = exact(expand[...], sums)
    scale = 1.0 / (ext * ext)
    spec_re[...] = (full[:BAND, :BAND] - full[BAND:, BAND:]) * scale
    spec_im[...] = (full[BAND:, :BAND] + full[:BAND, BAND:]) * -scale

    pl.when(has_up)(to_up.wait_send)
    pl.when(has_down)(to_down.wait_send)
    pl.when(has_left)(to_left.wait_send)
    pl.when(has_right)(to_right.wait_send)
    swap_weights.wait()
    swap_spectra.wait()


def image_kernel(
    spec_re, spec_im, spectra, other_spectra, weights, other_weights, first, second, flip,
    site_rows, site_cols, tolerance,
    intensity, edge_errors, peaks, shares,
    plus, minus, image, image_in, errors, errors_in, near, far, near_send, near_recv, far_send, far_recv,
):
    tx, ty, ka = lax.axis_index("tx"), lax.axis_index("ty"), lax.axis_index("ka")
    n_tx, n_ty, n_ka = lax.axis_size("tx"), lax.axis_size("ty"), lax.axis_size("ka")
    n_near = n_ty * n_ka
    place = ty * n_ka + ka
    barrier = pltpu.get_barrier_semaphore()

    def near_peer(d):
        spot = lax.rem(place + d, n_near)
        return spot, {"ty": spot // n_ka, "ka": lax.rem(spot, n_ka)}

    def far_peer(d):
        spot = lax.rem(tx + d, n_tx)
        return spot, {"tx": spot}

    for d in range(1, n_near):
        pl.semaphore_signal(barrier, inc=1, device_id=near_peer(d)[1], device_id_type=MESH)
    for d in range(1, n_tx):
        pl.semaphore_signal(barrier, inc=1, device_id=far_peer(d)[1], device_id_type=MESH)

    half = BAND
    re, im = spec_re[...], spec_im[...]
    plus[...] = jnp.zeros_like(plus)
    minus[...] = jnp.zeros_like(minus)

    def outer(y):
        hi, mid, lo = bf16_pieces(y, 3)
        upper, lower = jnp.concatenate([hi, mid], axis=0), jnp.concatenate([hi, lo], axis=0)
        return dot(second[0], upper) + dot(second[1], upper) + dot(second[2], lower)

    def add(kernels, k, weight):
        k_re, k_im = kernels[k, 0], kernels[k, 1]
        product = jnp.concatenate([k_re * re - k_im * im, k_re * im + k_im * re], axis=0)
        hi, mid, lo = bf16_pieces(product, 3)
        upper, lower = jnp.concatenate([hi, mid], axis=1), jnp.concatenate([hi, lo], axis=1)
        inner = dot(upper, first[0]) + dot(upper, first[1]) + dot(lower, first[2])
        a, c, d, b = inner[:half, :half], inner[:half, half:], inner[half:, :half], inner[half:, half:]
        y_re = jnp.concatenate([a - b, a + b], axis=1)
        y_im = jnp.concatenate([c + d, d - c], axis=1)
        of_re, of_im = outer(y_re), outer(y_im)
        a, c, d, b = of_re[:half], of_re[half:], of_im[:half], of_im[half:]
        p_re, p_im, m_re, m_im = a - b, c + d, a + b, d - c
        plus[...] += weight * (p_re * p_re + p_im * p_im)
        minus[...] += weight * (m_re * m_re + m_im * m_im)

    @pl.loop(0, spectra.shape[0])
    def _(k):
        add(spectra, k, weights[k])
        add(other_spectra, k, other_weights[pl.ds(k, 1), :])

    both = jnp.concatenate([exact(flip[...], minus[...]), plus[...]], axis=0)
    picture = jnp.concatenate([exact(both[:, half:], flip[...]), both[:, :half]], axis=1)
    image[...] = picture
    tile = picture.shape[0]
    grad_rows = (pltpu.roll(picture, tile - 1, 0) - pltpu.roll(picture, 1, 0)) * 0.5
    grad_cols = (pltpu.roll(picture, tile - 1, 1) - pltpu.roll(picture, 1, 1)) * 0.5
    slope = jnp.sqrt(grad_rows * grad_rows + grad_cols * grad_cols)
    field = (picture - LEVEL) / jnp.maximum(slope, SLOPE_FLOOR)
    field_hi, field_lo = bf16_pieces(field, 2)

    pl.semaphore_wait(barrier, n_near - 1 + n_tx - 1)

    def to_other(source, target, number):
        return pltpu.make_async_remote_copy(
            src_ref=source, dst_ref=target, send_sem=near_send.at[n_near + number],
            recv_sem=near_recv.at[n_near + number], device_id={"ka": 1 - ka}, device_id_type=MESH,
        )

    send_image = to_other(image, image_in, 0)
    send_errors = to_other(errors, errors_in, 1)
    send_image.start()

    width = tile
    place_at = lax.broadcasted_iota(jnp.int32, (tile, width), 0)
    for chunk in range(site_rows.shape[2] // width):
        at = slice(chunk * width, (chunk + 1) * width)
        wanted = jnp.where(place_at == site_cols[0, :, at], 1.0, 0.0).astype(jnp.bfloat16)
        sampled = dot(field_hi, wanted) + dot(field_lo, wanted)
        sampled = jnp.where(place_at == site_rows[0, :, at], sampled, 0.0)
        errors[:, at] = jnp.sum(sampled, axis=0, keepdims=True)

    found = errors[...]
    size = jnp.abs(found)
    limit = tolerance[ka].astype(jnp.float32) / 8.0
    peak = jnp.max(size, axis=1, keepdims=True)
    total = jnp.sum(1.0 / (1.0 + jnp.exp(SHARPNESS * (size - limit))), axis=1, keepdims=True)
    lane = lax.broadcasted_iota(jnp.int32, (1, 128), 1)
    is_peak = lane < 64
    near[place] = jnp.where(is_peak, peak, total)

    def small(buffer, mine, d, peer, send, recv):
        return pltpu.make_async_remote_copy(
            src_ref=buffer.at[mine], dst_ref=buffer.at[mine], send_sem=send.at[d], recv_sem=recv.at[mine],
            device_id=peer, device_id_type=MESH,
        )

    def swapped(buffer, mine, peers, send, recv):
        copies = [small(buffer, mine, d, peer, send, recv) for d, (_, peer) in peers]
        for copy in copies:
            copy.start()
        for d, (spot, peer) in peers:
            small(buffer, spot, d, peer, send, recv).wait_recv()
        return copies

    near_peers = [(d, near_peer(d)) for d in range(1, n_near)]
    far_peers = [(d, far_peer(d)) for d in range(1, n_tx)]
    copies = swapped(near, place, near_peers, near_send, near_recv)
    send_errors.start()
    of_iteration = []
    for t in range(n_ka):
        found_t = [near[y * n_ka + t] for y in range(n_ty)]
        of_iteration.append(
            jnp.where(is_peak, functools.reduce(jnp.maximum, found_t), functools.reduce(jnp.add, found_t))
        )
    far[tx] = jnp.where((lane & 32) == 0, of_iteration[0], of_iteration[1])
    copies += swapped(far, tx, far_peers, far_send, far_recv)
    final = jnp.where(is_peak, jnp.max(far[...], axis=0), jnp.sum(far[...], axis=0))
    share = 1.0 / float(site_rows.shape[2] * n_tx * n_ty)
    for t in range(ITERS):
        peaks[t] = final[0, 32 * t]
        shares[t] = final[0, 64 + 32 * t] * share

    send_image.wait()
    send_errors.wait()
    intensity[...] = jnp.where(ka == ITERS - 1, image[...], image_in[...])
    edge_errors[0, 0, 0:1, :] = jnp.where(ka == 0, errors[...], errors_in[...])
    edge_errors[0, 0, 1:2, :] = jnp.where(ka == 0, errors_in[...], errors[...])
    for copy in copies:
        copy.wait_send()


def shards(
    mask_raster, frag_rows, frag_cols, frag_length, frag_orient, frag_moves,
    site_rows, site_cols, spectra, weights, tolerance,
):
    f32 = jnp.float32
    tile = mask_raster.shape[0]
    half = tile // 2
    sites = site_rows.shape[2]
    kernels = spectra.shape[0]
    n_near = lax.axis_size("ty") * lax.axis_size("ka")
    n_tx = lax.axis_size("tx")
    row_dft, col_dft, expand, first, second, flip = (jnp.asarray(t) for t in tables(tile))
    vmem = pl.BlockSpec(memory_space=pltpu.VMEM)
    smem = pl.BlockSpec(memory_space=pltpu.SMEM)
    anywhere = pl.BlockSpec(memory_space=pl.ANY)
    dma = pltpu.SemaphoreType.DMA
    new_mask, spec_re, spec_im, other_spectra, other_weights = pl.pallas_call(
        halo_kernel,
        name="halo_kernel",
        out_shape=(
            jax.ShapeDtypeStruct((tile, tile), f32),
            jax.ShapeDtypeStruct((BAND, BAND), f32),
            jax.ShapeDtypeStruct((BAND, BAND), f32),
            jax.ShapeDtypeStruct(spectra.shape, f32),
            jax.ShapeDtypeStruct((kernels, tile), f32),
        ),
        in_specs=[vmem] * 6 + [anywhere, smem] + [vmem] * 3,
        out_specs=(vmem, vmem, vmem, anywhere, anywhere),
        scratch_shapes=[
            pltpu.VMEM((tile, tile), f32),
            pltpu.VMEM((HALO, tile), f32),
            pltpu.VMEM((HALO, tile), f32),
            pltpu.VMEM((PACKED, tile), f32),
            pltpu.VMEM((PACKED, HALO), f32),
            pltpu.VMEM((PACKED, HALO), f32),
            pltpu.VMEM((kernels, tile), f32),
            dma((6,)),
            dma((6,)),
        ],
        compiler_params=pltpu.CompilerParams(
            collective_id=0, has_side_effects=True, vmem_limit_bytes=16 * 2**20
        ),
        cost_estimate=pl.CostEstimate(flops=2 * 10**9, bytes_accessed=4 * 10**6, transcendentals=0),
    )(
        mask_raster, frag_rows, frag_cols, frag_length, frag_orient, frag_moves, spectra, weights,
        row_dft, col_dft, expand,
    )
    intensity, edge_errors, peaks, shares = pl.pallas_call(
        image_kernel,
        name="image_kernel",
        out_shape=(
            jax.ShapeDtypeStruct((tile, tile), f32),
            jax.ShapeDtypeStruct((1, 1, ITERS, sites), f32),
            jax.ShapeDtypeStruct((ITERS,), f32),
            jax.ShapeDtypeStruct((ITERS,), f32),
        ),
        in_specs=[vmem] * 4 + [smem] + [vmem] * 6 + [smem],
        out_specs=(vmem, vmem, smem, smem),
        scratch_shapes=[
            pltpu.VMEM((half, tile), f32),
            pltpu.VMEM((half, tile), f32),
            pltpu.VMEM((tile, tile), f32),
            pltpu.VMEM((tile, tile), f32),
            pltpu.VMEM((1, sites), f32),
            pltpu.VMEM((1, sites), f32),
            pltpu.VMEM((n_near, 1, 128), f32),
            pltpu.VMEM((n_tx, 1, 128), f32),
            dma((n_near + 2,)),
            dma((n_near + 2,)),
            dma((n_tx,)),
            dma((n_tx,)),
        ],
        compiler_params=pltpu.CompilerParams(
            collective_id=1, has_side_effects=True, vmem_limit_bytes=24 * 2**20
        ),
        cost_estimate=pl.CostEstimate(flops=4 * 10**9, bytes_accessed=4 * 10**6, transcendentals=0),
    )(
        spec_re, spec_im, spectra, other_spectra, weights, other_weights, first, second, flip,
        site_rows, site_cols, tolerance,
    )
    return intensity, new_mask, edge_errors, peaks, shares


def solution(mesh):
    placed = (
        P(("groups", "tx"), "ty"),
        P(("groups", "tx"), "ty", None),
        P(("groups", "tx"), "ty", None),
        P(("groups", "tx"), "ty", None),
        P(("groups", "tx"), "ty", None),
        P(("groups", "tx"), "ty", None, None),
        P(("groups", "tx"), "ty", None),
        P(("groups", "tx"), "ty", None),
        P("ka", None, None, None),
        P("ka"),
        P(),
    )
    return jax.shard_map(
        shards,
        mesh=mesh,
        in_specs=placed,
        out_specs=(
            P(("groups", "tx"), "ty"),
            P(("groups", "tx"), "ty"),
            P(("groups", "tx"), "ty", None, None),
            P("groups"),
            P("groups"),
        ),
        check_vma=False,
    )
```

profile of v0, /device:TPU:33, one launch (start us, length us, event | category | flops | bytes accessed | tf_op | source)
XLA Modules:
  0.0 70.6 jit_solution(2013742598613119303)
XLA Ops:
  0.6 1.2 %copy-done = f32[8,2,128,128]{3,2,1,0:T(8,128)S(1)} copy-done((f32[8,2,128,128]{3,2,1,0:T(8,128)S(1)}, f32[8,2,128,128]{3,2,1,0:T(8,128)}, u32[]{:S(2)}) %copy-start) | copy-done | bytes 1048600
  1.9 0.9 %copy-done.2 = f32[256,256]{1,0:T(8,128)S(1)} copy-done((f32[256,256]{1,0:T(8,128)S(1)}, f32[256,256]{1,0:T(8,128)}, u32[]{:S(2)}) %copy-start.2) | copy-done | bytes 262168
  2.8 0.7 copy-done.5
  3.5 0.7 copy-done.6
  4.2 0.7 copy-done.7
  4.9 0.7 copy-done.8
  5.5 0.7 copy-done.9
  6.2 0.7 copy-done.10
  6.9 1.0 %copy-done.13 = f32[512,256]{1,0:T(8,128)S(1)} copy-done((f32[512,256]{1,0:T(8,128)S(1)}, f32[512,256]{1,0:T(8,128)}, u32[]{:S(2)}) %copy-start.13) | copy-done | bytes 524312
  7.9 1.0 %copy-done.16 = f32[136,512]{1,0:T(8,128)S(1)} copy-done((f32[136,512]{1,0:T(8,128)S(1)}, f32[136,512]{1,0:T(8,128)}, u32[]{:S(2)}) %copy-start.16) | copy-done | bytes 278552
  8.9 0.9 %copy-done.17 = f32[256,136]{1,0:T(8,128)S(1)} copy-done((f32[256,136]{1,0:T(8,128)S(1)}, f32[256,136]{1,0:T(8,128)}, u32[]{:S(2)}) %copy-start.17) | copy-done | bytes 139288
  9.8 0.0 copy-start.18
  9.9 24.0 %halo_kernel.1 = (f32[256,256]{1,0:T(8,128)S(1)}, f32[128,128]{1,0:T(8,128)S(1)}, f32[128,128]{1,0:T(8,128)S(1)}, f32[8,2,128,128]{3,2,1,0:T(8,128)S(1)}, f32[8,256]{1,0:T(8,128)S(1)}) custom-call(f32[256,256]{1,0:T(8,128)S(1)} %copy-done.2, s32[1,1,512]{2,1,0:T(1,128)S(1)} %copy-done.6, s32[1,1,512]{2,1,0:T(1,128)S(1)} %copy-done.7, ...), custom_call_target="tpu_custom_call" | custom-call | flops 2000000000 | bytes 4000000 | tf_op jit(solution)/shard_map/halo_kernel/pallas_call | solution.py:322
  33.9 0.0 copy-start.3
  33.9 0.0 copy-start.11
  33.9 0.0 copy-start.12
  33.9 0.0 copy-done.1
  34.0 0.6 copy-done.3
  34.6 33.0 %image_kernel.1 = (f32[256,256]{1,0:T(8,128)S(1)}, f32[1,1,2,2048]{3,2,1,0:T(2,128)S(1)}, f32[2]{0:T(128)S(1)}, f32[2]{0:T(128)S(1)}) custom-call(f32[128,128]{1,0:T(8,128)S(1)} %get-tuple-element.14.spec_re, f32[128,128]{1,0:T(8,128)S(1)} %get-tuple-element.15.spec_im, f32[8,2,128,128]{3,2,1,0:T(8,128)S(1)} %copy-done.1, ...), custom_call_target="tpu_custom_call" | custom-call | flops 4000000000 | bytes 4000000 | tf_op jit(solution)/shard_map/image_kernel/pallas_call | solution.py:353
  67.6 0.7 copy.27
  68.3 0.7 copy.28
  69.0 0.6 copy.29
  69.6 0.5 copy.30
  70.1 0.5 copy.31
  (21 shorter events, 0.0 us)
Async XLA Ops:
  0.6 1.2 %copy-start = (f32[8,2,128,128]{3,2,1,0:T(8,128)S(1)}, f32[8,2,128,128]{3,2,1,0:T(8,128)}, u32[]{:S(2)}) copy-start(f32[8,2,128,128]{3,2,1,0:T(8,128)} %spectra.3) | copy-start | bytes 3145732
  1.9 0.9 %copy-start.2 = (f32[256,256]{1,0:T(8,128)S(1)}, f32[256,256]{1,0:T(8,128)}, u32[]{:S(2)}) copy-start(f32[256,256]{1,0:T(8,128)} %mask.1) | copy-start | bytes 786436
  2.8 0.7 copy-start.5
  3.5 0.7 copy-start.6
  4.2 0.7 copy-start.7
  4.9 0.7 copy-start.8
  5.5 0.7 copy-start.9
  6.2 0.7 copy-start.10
  6.9 1.0 %copy-start.13 = (f32[512,256]{1,0:T(8,128)S(1)}, f32[512,256]{1,0:T(8,128)}, u32[]{:S(2)}) copy-start(f32[512,256]{1,0:T(8,128)} %constant.13.clone.col_dft) | copy-start | bytes 1572868
  7.9 1.0 %copy-start.16 = (f32[136,512]{1,0:T(8,128)S(1)}, f32[136,512]{1,0:T(8,128)}, u32[]{:S(2)}) copy-start(f32[136,512]{1,0:T(8,128)} %constant.12.clone.row_dft) | copy-start | bytes 835588
  8.9 0.9 %copy-start.17 = (f32[256,136]{1,0:T(8,128)S(1)}, f32[256,136]{1,0:T(8,128)}, u32[]{:S(2)}) copy-start(f32[256,136]{1,0:T(8,128)} %constant.14.clone.expand) | copy-start | bytes 417796
  9.8 24.1 %copy-start.1 = (f32[8,2,128,128]{3,2,1,0:T(8,128)S(1)}, f32[8,2,128,128]{3,2,1,0:T(8,128)}, u32[]{:S(2)}) copy-start(f32[8,2,128,128]{3,2,1,0:T(8,128)} %spectra.3) | copy-start | bytes 3145732
  9.8 24.1 %copy-start.4 = (s32[1,1,2048]{2,1,0:T(1,128)S(1)}, s32[1,1,2048]{2,1,0:T(1,128)}, u32[]{:S(2)}) copy-start(s32[1,1,2048]{2,1,0:T(1,128)} %site_cols.1) | copy-start | bytes 24580
  9.8 24.1 %copy-start.14 = (bf16[3,256,256]{2,1,0:T(8,128)(2,1)S(1)}, bf16[3,256,256]{2,1,0:T(8,128)(2,1)}, u32[]{:S(2)}) copy-start(bf16[3,256,256]{2,1,0:T(8,128)(2,1)} %constant.16.clone.second) | copy-start | bytes 1179652
  9.8 24.1 %copy-start.15 = (bf16[3,256,256]{2,1,0:T(8,128)(2,1)S(1)}, bf16[3,256,256]{2,1,0:T(8,128)(2,1)}, u32[]{:S(2)}) copy-start(bf16[3,256,256]{2,1,0:T(8,128)(2,1)} %constant.15.clone.first) | copy-start | bytes 1179652
  9.8 24.1 %copy-start.18 = (f32[128,128]{1,0:T(8,128)S(1)}, f32[128,128]{1,0:T(8,128)}, u32[]{:S(2)}) copy-start(f32[128,128]{1,0:T(8,128)} %constant.17.clone.flip) | copy-start | bytes 196612
  33.9 0.7 copy-start.3
  33.9 0.7 copy-start.11
  33.9 0.7 copy-start.12
where the time goes:
time: 71.2 us; the launch traced here: 70.6 us
  Pallas kernels  57 us (80%)
  local copies, waits for them, and re-layouts  12.9 us (18%)
  between operations  0.75 us (1%)
    pallas_call x1, Pallas kernels, shards(): pl.pallas_call(image_kernel, name='image_kernel', out_shape=(jax.ShapeDty...  33 us
    pallas_call x1, Pallas kernels, shards(): pl.pallas_call(halo_kernel, name='halo_kernel', out_shape=(jax.ShapeDtype...  24 us
    unnamed x43, local copies, waits for them, and re-layouts  12.9 us

commit v1 on v0

v1 whole, which is shorter than its diff:
```python
import functools
import math

import jax
import jax.numpy as jnp
import numpy as np
from jax import lax
from jax.experimental import pallas as pl
from jax.experimental.pallas import tpu as pltpu
from jax.sharding import PartitionSpec as P

HALO = 128
BAND = 128
ITERS = 2
LEVEL = 0.4
SLOPE_FLOOR = 0.05
SHARPNESS = 8.0
HIGHEST = lax.Precision.HIGHEST
MESH = pl.DeviceIdType.MESH
SIN_AT = 72
PACKED = 136


def bf16_pieces(x, count):
    pieces = []
    for _ in range(count):
        pieces.append(x.astype(jnp.bfloat16))
        x = x - pieces[-1].astype(jnp.float32)
    return pieces


def host_pieces(x):
    pieces = []
    for _ in range(3):
        pieces.append(x.astype(jnp.bfloat16))
        x = x - pieces[-1].astype(np.float64)
    return pieces


def tables(tile):
    ext = tile + 2 * HALO
    half = tile // 2
    theta = 2.0 * math.pi / ext
    inside = np.arange(ext) - (ext - 1) / 2
    low = BAND // 2
    rows = np.zeros((PACKED, ext))
    rows[: low + 1] = np.cos(theta * np.outer(np.arange(low + 1), inside))
    rows[SIN_AT : SIN_AT + low] = np.sin(theta * np.outer(np.arange(1, low + 1), inside))
    freq = np.arange(BAND) - low
    turns = theta * np.outer(inside, freq)
    cols = np.concatenate([np.cos(turns), np.sin(turns)], axis=1)
    expand = np.zeros((2 * BAND, PACKED))
    for u, f in enumerate(freq):
        expand[u, abs(f)] = 1.0
        if f != 0:
            expand[BAND + u, SIN_AT + abs(f) - 1] = np.sign(f)
    out = theta * np.outer(freq, np.arange(half) + 0.5)
    basis = np.concatenate([np.cos(out), np.sin(out)], axis=1)
    hi, mid, lo = host_pieces(basis)
    first = np.stack([np.concatenate(b, axis=0) for b in ((hi, hi), (mid, mid), (lo, hi))])
    second = np.ascontiguousarray(first.swapaxes(1, 2))
    flip = np.eye(half)[::-1]
    f32 = np.float32
    return rows.astype(f32), cols.astype(f32), expand.astype(f32), first, second, flip.astype(f32)


def exact(left, right):
    return jnp.dot(left, right, precision=HIGHEST, preferred_element_type=jnp.float32)


def dot(left, right):
    return jnp.dot(left, right, preferred_element_type=jnp.float32)


def opc_kernel(
    mask, rows_at, cols_at, lengths, orients, moves, site_rows, site_cols, spectra, weights, tolerance,
    row_dft_in, col_dft_in, expand_in, first_in, second_in, flip_in,
    new_mask, intensity, edge_errors, stats,
    current, fragments, frag_moves, sites, kernels, my_weights, other_weights, weight_of, limits,
    row_dft, col_dft, expand, first, second, flip,
    above, below, packed, left, right, spec_re, spec_im, wanted,
    plus, minus, image, image_in, errors, errors_in, near, far, mask_out, image_out, errors_out, stats_out,
    load_sem, save_sem, halo_send, halo_recv, near_send, near_recv, far_send, far_recv, ready,
):
    tx, ty, ka = lax.axis_index("tx"), lax.axis_index("ty"), lax.axis_index("ka")
    n_tx, n_ty, n_ka = lax.axis_size("tx"), lax.axis_size("ty"), lax.axis_size("ka")
    n_near = n_ty * n_ka
    place = ty * n_ka + ka
    tile = mask.shape[0]
    ext = tile + 2 * HALO
    half = tile // 2
    has_up, has_down = tx > 0, tx < n_tx - 1
    has_left, has_right = ty > 0, ty < n_ty - 1

    pairs = [
        (mask, current), (rows_at, fragments.at[0]), (cols_at, fragments.at[1]), (lengths, fragments.at[2]),
        (orients, fragments.at[3]), (moves, frag_moves), (weights, weight_of), (row_dft_in, row_dft),
        (site_cols, sites.at[0]), (col_dft_in, col_dft), (expand_in, expand), (spectra, kernels.at[0]),
        (first_in, first), (second_in, second), (flip_in, flip), (site_rows, sites.at[1]), (tolerance, limits),
    ]
    loads = [pltpu.make_async_copy(src, dst, load_sem.at[i]) for i, (src, dst) in enumerate(pairs)]
    for load in loads:
        load.start()

    def near_peer(d):
        spot = lax.rem(place + d, n_near)
        return spot, {"ty": spot // n_ka, "ka": lax.rem(spot, n_ka)}

    def far_peer(d):
        spot = lax.rem(tx + d, n_tx)
        return spot, {"tx": spot}

    barrier = pltpu.get_barrier_semaphore()
    for d in range(1, n_near):
        pl.semaphore_signal(barrier, inc=1, device_id=near_peer(d)[1], device_id_type=MESH)

    @pl.when(has_up)
    def _():
        pl.semaphore_signal(barrier, inc=1, device_id={"tx": tx - 1}, device_id_type=MESH)

    for d in range(1, n_tx):
        @pl.when(tx + d < n_tx)
        def _():
            pl.semaphore_signal(barrier, inc=1, device_id={"tx": tx + d}, device_id_type=MESH)

    for load in loads[:7]:
        load.wait()
    position = lax.broadcasted_iota(jnp.int32, (tile, rows_at.shape[2]), 0)
    row, col, length = fragments[0, 0], fragments[1, 0], fragments[2, 0]
    along = fragments[3, 0] == 0
    steps = [current[...]]
    for t in range(ITERS):
        move = frag_moves[0, 0, t : t + 1, :]
        lower, upper = jnp.minimum(move, 0), jnp.maximum(move, 0)
        row_low = jnp.where(along, row, row + lower)
        row_high = jnp.where(along, row + length, row + upper)
        col_low = jnp.where(along, col + lower, col)
        col_high = jnp.where(along, col + upper, col + length)
        sign = jnp.where(move > 0, 1.0, 0.0) - jnp.where(move < 0, 1.0, 0.0)
        in_rows = jnp.where((position >= row_low) & (position < row_high), sign, 0.0)
        in_cols = jnp.where((position >= col_low) & (position < col_high), 1.0, 0.0)
        strips = lax.dot_general(
            in_rows.astype(jnp.bfloat16), in_cols.astype(jnp.bfloat16), (((1,), (1,)), ((), ())),
            preferred_element_type=jnp.float32,
        )
        steps.append(jnp.clip(steps[-1] + strips, 0.0, 1.0))
    mask_out[...] = steps[2]
    current[...] = jnp.where(ka == 0, steps[1], steps[2])
    for k in range(my_weights.shape[0]):
        my_weights[pl.ds(k, 1), :] = jnp.full((1, my_weights.shape[1]), weight_of[k], jnp.float32)

    pl.semaphore_wait(barrier, n_near - 1 + tx + has_down.astype(jnp.int32))

    def hop(source, target, number, device):
        return pltpu.make_async_remote_copy(
            src_ref=source, dst_ref=target, send_sem=halo_send.at[number], recv_sem=halo_recv.at[number],
            device_id=device, device_id_type=MESH,
        )

    to_up = hop(current.at[pl.ds(0, half)], below, 0, {"tx": tx - 1})
    to_down = hop(current.at[pl.ds(half, half)], above, 1, {"tx": tx + 1})
    to_left = hop(packed.at[:, pl.ds(0, half)], right, 2, {"ty": ty - 1})
    to_right = hop(packed.at[:, pl.ds(half, half)], left, 3, {"ty": ty + 1})
    swap_weights = hop(my_weights, other_weights, 4, {"ka": 1 - ka})
    swap_spectra = hop(spectra, kernels.at[1], 5, {"ka": 1 - ka})
    pl.when(has_up)(to_up.start)
    pl.when(has_down)(to_down.start)
    swap_spectra.start()
    swap_weights.start()
    pairs = ((mask_out, new_mask), (image_out, intensity), (errors_out, edge_errors), (stats_out, stats))
    saves = [pltpu.make_async_copy(src, dst, save_sem.at[i]) for i, (src, dst) in enumerate(pairs)]
    saves[0].start()
    for d in range(1, n_tx):
        @pl.when(tx - d >= 0)
        def _():
            pl.semaphore_signal(ready, inc=1, device_id={"tx": tx - d}, device_id_type=MESH)

    def arrived(there, copy, buffer):
        pl.when(there)(copy.wait_recv)

        @pl.when(jnp.logical_not(there))
        def _():
            buffer[...] = jnp.zeros_like(buffer)

    loads[7].wait()
    part = exact(row_dft[:, HALO : HALO + tile], current[...])
    loads[8].wait()
    place_at = lax.broadcasted_iota(jnp.int32, (tile, tile), 0)
    chunks = site_rows.shape[2] // tile
    for chunk in range(chunks):
        at = slice(chunk * tile, (chunk + 1) * tile)
        wanted[:, at] = jnp.where(place_at == sites[0, 0, :, at], 1.0, 0.0).astype(jnp.bfloat16)
    for load in loads[9:]:
        load.wait()
    arrived(has_up, to_down, above)
    arrived(has_down, to_up, below)
    part = part + exact(row_dft[:, :HALO], above[...]) + exact(row_dft[:, HALO + tile :], below[...])
    packed[...] = part
    pl.when(has_left)(to_left.start)
    pl.when(has_right)(to_right.start)
    sums = exact(part, col_dft[HALO : HALO + tile, :])
    plus[...] = jnp.zeros_like(plus)
    minus[...] = jnp.zeros_like(minus)
    swap_weights.wait()
    swap_spectra.wait()
    arrived(has_left, to_right, left)
    arrived(has_right, to_left, right)
    sums = sums + exact(left[...], col_dft[:HALO, :]) + exact(right[...], col_dft[HALO + tile :, :])
    full = exact(expand[...], sums)
    scale = 1.0 / (ext * ext)
    spec_re[...] = (full[:BAND, :BAND] - full[BAND:, BAND:]) * scale
    spec_im[...] = (full[BAND:, :BAND] + full[:BAND, BAND:]) * -scale

    def outer(y):
        hi, mid, lo = bf16_pieces(y, 3)
        upper, lower = jnp.concatenate([hi, mid], axis=0), jnp.concatenate([hi, lo], axis=0)
        return dot(second[0], upper) + dot(second[1], upper) + dot(second[2], lower)

    def add(k_re, k_im, weight):
        re, im = spec_re[...], spec_im[...]
        product = jnp.concatenate([k_re * re - k_im * im, k_re * im + k_im * re], axis=0)
        hi, mid, lo = bf16_pieces(product, 3)
        upper, lower = jnp.concatenate([hi, mid], axis=1), jnp.concatenate([hi, lo], axis=1)
        inner = dot(upper, first[0]) + dot(upper, first[1]) + dot(lower, first[2])
        a, c, d, b = inner[:half, :half], inner[:half, half:], inner[half:, :half], inner[half:, half:]
        y_re = jnp.concatenate([a - b, a + b], axis=1)
        y_im = jnp.concatenate([c + d, d - c], axis=1)
        of_re, of_im = outer(y_re), outer(y_im)
        a, c, d, b = of_re[:half], of_re[half:], of_im[:half], of_im[half:]
        p_re, p_im, m_re, m_im = a - b, c + d, a + b, d - c
        plus[...] += weight * (p_re * p_re + p_im * p_im)
        minus[...] += weight * (m_re * m_re + m_im * m_im)

    @pl.loop(0, spectra.shape[0])
    def _(k):
        add(kernels[0, k, 0], kernels[0, k, 1], my_weights[pl.ds(k, 1), :])
        add(kernels[1, k, 0], kernels[1, k, 1], other_weights[pl.ds(k, 1), :])

    both = jnp.concatenate([exact(flip[...], minus[...]), plus[...]], axis=0)
    picture = jnp.concatenate([exact(both[:, half:], flip[...]), both[:, :half]], axis=1)
    image[...] = picture
    grad_rows = (pltpu.roll(picture, tile - 1, 0) - pltpu.roll(picture, 1, 0)) * 0.5
    grad_cols = (pltpu.roll(picture, tile - 1, 1) - pltpu.roll(picture, 1, 1)) * 0.5
    slope = jnp.sqrt(grad_rows * grad_rows + grad_cols * grad_cols)
    field = (picture - LEVEL) / jnp.maximum(slope, SLOPE_FLOOR)
    field_hi, field_lo = bf16_pieces(field, 2)

    def to_other(source, target, number):
        return pltpu.make_async_remote_copy(
            src_ref=source, dst_ref=target, send_sem=near_send.at[n_near + number],
            recv_sem=near_recv.at[n_near + number], device_id={"ka": 1 - ka}, device_id_type=MESH,
        )

    send_image = to_other(image, image_in, 0)
    send_errors = to_other(errors, errors_in, 1)
    send_image.start()

    for chunk in range(chunks):
        at = slice(chunk * tile, (chunk + 1) * tile)
        sampled = dot(field_hi, wanted[:, at]) + dot(field_lo, wanted[:, at])
        sampled = jnp.where(place_at == sites[1, 0, :, at], sampled, 0.0)
        errors[:, at] = jnp.sum(sampled, axis=0, keepdims=True)

    found = errors[...]
    size = jnp.abs(found)
    limit = limits[ka].astype(jnp.float32) / 8.0
    peak = jnp.max(size, axis=1, keepdims=True)
    total = jnp.sum(1.0 / (1.0 + jnp.exp(SHARPNESS * (size - limit))), axis=1, keepdims=True)
    lane = lax.broadcasted_iota(jnp.int32, (1, 128), 1)
    is_peak = lane < 64
    near[place] = jnp.where(is_peak, peak, total)

    def small(buffer, mine, d, peer, send, recv):
        return pltpu.make_async_remote_copy(
            src_ref=buffer.at[mine], dst_ref=buffer.at[mine], send_sem=send.at[d], recv_sem=recv.at[mine],
            device_id=peer, device_id_type=MESH,
        )

    def swapped(buffer, mine, peers, send, recv):
        copies = [small(buffer, mine, d, peer, send, recv) for d, (_, peer) in peers]
        for copy in copies:
            copy.start()
        for d, (spot, peer) in peers:
            small(buffer, spot, d, peer, send, recv).wait_recv()
        return copies

    near_peers = [(d, near_peer(d)) for d in range(1, n_near)]
    far_peers = [(d, far_peer(d)) for d in range(1, n_tx)]

    @pl.when(has_down)
    def _():
        pl.semaphore_wait(ready, n_tx - 1 - tx)

    copies = swapped(near, place, near_peers, near_send, near_recv)
    of_iteration = []
    for t in range(n_ka):
        found_t = [near[y * n_ka + t] for y in range(n_ty)]
        of_iteration.append(
            jnp.where(is_peak, functools.reduce(jnp.maximum, found_t), functools.reduce(jnp.add, found_t))
        )
    far[tx] = jnp.where((lane & 32) == 0, of_iteration[0], of_iteration[1])
    far_copies = [small(far, tx, d, peer, far_send, far_recv) for d, (_, peer) in far_peers]
    for copy in far_copies:
        copy.start()
    send_errors.start()
    send_image.wait()
    send_errors.wait()
    image_out[...] = jnp.where(ka == ITERS - 1, image[...], image_in[...])
    errors_out[0, 0, 0:1, :] = jnp.where(ka == 0, errors[...], errors_in[...])
    errors_out[0, 0, 1:2, :] = jnp.where(ka == 0, errors_in[...], errors[...])
    saves[1].start()
    saves[2].start()
    pl.when(has_up)(to_up.wait_send)
    pl.when(has_down)(to_down.wait_send)
    pl.when(has_left)(to_left.wait_send)
    pl.when(has_right)(to_right.wait_send)
    for copy in copies:
        copy.wait_send()
    for d, (spot, peer) in far_peers:
        small(far, spot, d, peer, far_send, far_recv).wait_recv()
    stats_out[...] = jnp.where(is_peak, jnp.max(far[...], axis=0), jnp.sum(far[...], axis=0))
    saves[3].start()
    for copy in far_copies:
        copy.wait_send()
    for save in saves:
        save.wait()


def deliver_kernel(
    n_sites, image, mask, errors, stats, intensity, new_mask, edge_errors, peaks, shares,
    image_at, mask_at, errors_at, stats_at, sem,
):
    held = ((stats, stats_at, None), (image, image_at, intensity), (mask, mask_at, new_mask), (errors, errors_at, edge_errors))
    loads = [pltpu.make_async_copy(src, at, sem.at[0, i]) for i, (src, at, _) in enumerate(held)]
    copies = [pltpu.make_async_copy(at, dst, sem.at[1, i]) for i, (_, at, dst) in enumerate(held) if i > 0]
    for load in loads:
        load.start()
    loads[0].wait()
    for load, copy in zip(loads[1:], copies):
        load.wait()
        copy.start()
    final = stats_at[...]
    for t in range(ITERS):
        peaks[t] = final[0, 32 * t]
        shares[t] = final[0, 64 + 32 * t] * (1.0 / n_sites)
    for copy in copies:
        copy.wait()


def shards(
    mask_raster, frag_rows, frag_cols, frag_length, frag_orient, frag_moves,
    site_rows, site_cols, spectra, weights, tolerance,
):
    f32, i32, bf16 = jnp.float32, jnp.int32, jnp.bfloat16
    tile = mask_raster.shape[0]
    half = tile // 2
    n_sites = site_rows.shape[2]
    kernels = spectra.shape[0]
    n_near = lax.axis_size("ty") * lax.axis_size("ka")
    n_tx = lax.axis_size("tx")
    constants = [jnp.asarray(t) for t in tables(tile)]
    smem = pl.BlockSpec(memory_space=pltpu.SMEM)
    hbm = pl.BlockSpec(memory_space=pltpu.HBM)
    dma = pltpu.SemaphoreType.DMA
    errors_shape = jax.ShapeDtypeStruct((1, 1, ITERS, n_sites), f32)
    square = jax.ShapeDtypeStruct((tile, tile), f32)
    V = pltpu.VMEM
    new_mask, image, errors, stats = pl.pallas_call(
        opc_kernel,
        name="opc_kernel",
        out_shape=(square, square, errors_shape, jax.ShapeDtypeStruct((1, 128), f32)),
        in_specs=[hbm] * 17,
        out_specs=(hbm,) * 4,
        scratch_shapes=[
            V((tile, tile), f32), V((4, *frag_rows.shape), i32), V(frag_moves.shape, i32),
            V((2, *site_rows.shape), i32), V((2, *spectra.shape), f32), V((kernels, tile), f32),
            V((kernels, tile), f32), pltpu.SMEM(weights.shape, f32), pltpu.SMEM(tolerance.shape, i32),
            *(V(c.shape, c.dtype) for c in constants),
            V((HALO, tile), f32), V((HALO, tile), f32), V((PACKED, tile), f32),
            V((PACKED, HALO), f32), V((PACKED, HALO), f32), V((BAND, BAND), f32), V((BAND, BAND), f32),
            V((tile, n_sites), bf16),
            V((half, tile), f32), V((half, tile), f32), V((tile, tile), f32), V((tile, tile), f32),
            V((1, n_sites), f32), V((1, n_sites), f32), V((n_near, 1, 128), f32), V((n_tx, 1, 128), f32),
            V((tile, tile), f32), V((tile, tile), f32), V(errors_shape.shape, f32), V((1, 128), f32),
            dma((17,)), dma((4,)), dma((6,)), dma((6,)), dma((n_near + 2,)), dma((n_near + 2,)), dma((n_tx,)), dma((n_tx,)),
            pltpu.SemaphoreType.REGULAR,
        ],
        compiler_params=pltpu.CompilerParams(collective_id=0, has_side_effects=True),
        cost_estimate=pl.CostEstimate(flops=4 * 10**9, bytes_accessed=4 * 10**6, transcendentals=0),
    )(
        mask_raster, frag_rows, frag_cols, frag_length, frag_orient, frag_moves, site_rows, site_cols,
        spectra, weights, tolerance, *constants,
    )
    pair = jax.ShapeDtypeStruct((ITERS,), f32)
    return pl.pallas_call(
        functools.partial(deliver_kernel, float(n_sites * n_tx * lax.axis_size("ty"))),
        name="deliver_kernel",
        out_shape=(square, square, errors_shape, pair, pair),
        in_specs=[hbm] * 4,
        out_specs=(hbm, hbm, hbm, smem, smem),
        scratch_shapes=[
            V((tile, tile), f32), V((tile, tile), f32), V(errors_shape.shape, f32), V((1, 128), f32), dma((2, 4)),
        ],
    )(image, new_mask, errors, stats)


def solution(mesh):
    placed = (
        P(("groups", "tx"), "ty"),
        P(("groups", "tx"), "ty", None),
        P(("groups", "tx"), "ty", None),
        P(("groups", "tx"), "ty", None),
        P(("groups", "tx"), "ty", None),
        P(("groups", "tx"), "ty", None, None),
        P(("groups", "tx"), "ty", None),
        P(("groups", "tx"), "ty", None),
        P("ka", None, None, None),
        P("ka"),
        P(),
    )
    return jax.shard_map(
        shards,
        mesh=mesh,
        in_specs=placed,
        out_specs=(
            P(("groups", "tx"), "ty"),
            P(("groups", "tx"), "ty"),
            P(("groups", "tx"), "ty", None, None),
            P("groups"),
            P("groups"),
        ),
        check_vma=False,
    )
```

time: 71.2 us -> 60.2 us (0.85)
  local copies, waits for them, and re-layouts: 12.9 us -> 0 us
  Pallas kernels: 57 us -> 59.4 us
    unnamed x43 -> x0, local copies, waits for them, and re-layouts: 12.9 us -> none
    pallas_call x2, Pallas kernels: 57 us -> 59.4 us  [the longest x1 57.1 us: shards(): pl.pallas_call(opc_kernel, name='opc_kernel', out_shape=(square, square,...]
where the time goes in v1:
time: 60.2 us; the launch traced here: 60.1 us
  Pallas kernels  59.4 us (99%)
  between operations  0.64 us (1%)
    pallas_call x1, Pallas kernels, shards(): pl.pallas_call(opc_kernel, name='opc_kernel', out_shape=(square, square,...  57.1 us
    pallas_call x1, Pallas kernels, shards(): pl.pallas_call(functools.partial(deliver_kernel, float(n_sites * n_tx * l...  2.34 us

profile of v1, /device:TPU:33, one launch (start us, length us, event | category | flops | bytes accessed | tf_op | source)
XLA Modules:
  0.0 60.1 jit_solution(4900067796544778583)
XLA Ops:
  0.6 57.1 %opc_kernel.1 = (f32[256,256]{1,0:T(8,128)}, f32[256,256]{1,0:T(8,128)}, f32[1,1,2,2048]{3,2,1,0:T(2,128)}, f32[1,128]{1,0:T(1,128)}) custom-call(f32[256,256]{1,0:T(8,128)} %mask.1, s32[1,1,512]{2,1,0:T(1,128)} %rows_at.1, s32[1,1,512]{2,1,0:T(1,128)} %cols_at.1, s32[1,1,512]{2,1,0:T(1,128)} %lengths.1, s32[1,1,512]{2,1,0:T(1,128)} %orients.1, ...), custom_call_target="tpu_custom_call" | custom-call | flops 4000000000 | bytes 4000000 | tf_op jit(solution)/shard_map/opc_kernel/pallas_call | solution.py:368
  57.7 2.3 %deliver_kernel.1 = (f32[256,256]{1,0:T(8,128)}, f32[256,256]{1,0:T(8,128)}, f32[1,1,2,2048]{3,2,1,0:T(2,128)}, f32[2]{0:T(128)}, f32[2]{0:T(128)}) custom-call(f32[256,256]{1,0:T(8,128)} %get-tuple-element.9.image, f32[256,256]{1,0:T(8,128)} %get-tuple-element.10.mask, f32[1,1,2,2048]{3,2,1,0:T(2,128)} %get-tuple-element.11.errors, ...), custom_call_target="tpu_custom_call" | custom-call | tf_op jit(solution)/shard_map/deliver_kernel/pallas_call | solution.py:395

commit v2 on v1

--- a/solution.py
+++ b/solution.py
@@ -80,7 +80,7 @@
     row_dft, col_dft, expand, first, second, flip,
     above, below, packed, left, right, spec_re, spec_im, wanted,
     plus, minus, image, image_in, errors, errors_in, near, far, mask_out, image_out, errors_out, stats_out,
-    load_sem, save_sem, halo_send, halo_recv, near_send, near_recv, far_send, far_recv, ready,
+    slot_a, slot_b, slot_c, slot_d, slot_e, slot_f, slot_g, slot_h, load_sem, save_sem, halo_send, halo_recv, near_send, near_recv, far_send, far_recv, token, ready,
 ):
     tx, ty, ka = lax.axis_index("tx"), lax.axis_index("ty"), lax.axis_index("ka")
     n_tx, n_ty, n_ka = lax.axis_size("tx"), lax.axis_size("ty"), lax.axis_size("ka")
@@ -89,6 +89,7 @@
     tile = mask.shape[0]
     ext = tile + 2 * HALO
     half = tile // 2
+    slots = ((slot_a, slot_b), (slot_c, slot_d), (slot_e, slot_f), (slot_g, slot_h))
     has_up, has_down = tx > 0, tx < n_tx - 1
     has_left, has_right = ty > 0, ty < n_ty - 1
 
@@ -118,10 +119,9 @@
     def _():
         pl.semaphore_signal(barrier, inc=1, device_id={"tx": tx - 1}, device_id_type=MESH)
 
-    for d in range(1, n_tx):
-        @pl.when(tx + d < n_tx)
-        def _():
-            pl.semaphore_signal(barrier, inc=1, device_id={"tx": tx + d}, device_id_type=MESH)
+    @pl.when(has_down)
+    def _():
+        pl.semaphore_signal(barrier, inc=1, device_id={"tx": tx + 1}, device_id_type=MESH)
 
     for load in loads[:7]:
         load.wait()
@@ -149,7 +149,7 @@
     for k in range(my_weights.shape[0]):
         my_weights[pl.ds(k, 1), :] = jnp.full((1, my_weights.shape[1]), weight_of[k], jnp.float32)
 
-    pl.semaphore_wait(barrier, n_near - 1 + tx + has_down.astype(jnp.int32))
+    pl.semaphore_wait(barrier, n_near - 1 + has_up.astype(jnp.int32) + has_down.astype(jnp.int32))
 
     def hop(source, target, number, device):
         return pltpu.make_async_remote_copy(
@@ -170,11 +170,6 @@
     pairs = ((mask_out, new_mask), (image_out, intensity), (errors_out, edge_errors), (stats_out, stats))
     saves = [pltpu.make_async_copy(src, dst, save_sem.at[i]) for i, (src, dst) in enumerate(pairs)]
     saves[0].start()
-    for d in range(1, n_tx):
-        @pl.when(tx - d >= 0)
-        def _():
-            pl.semaphore_signal(ready, inc=1, device_id={"tx": tx - d}, device_id_type=MESH)
-
     def arrived(there, copy, buffer):
         pl.when(there)(copy.wait_recv)
 
@@ -211,30 +206,48 @@
     spec_re[...] = (full[:BAND, :BAND] - full[BAND:, BAND:]) * scale
     spec_im[...] = (full[BAND:, :BAND] + full[:BAND, BAND:]) * -scale
 
-    def outer(y):
-        hi, mid, lo = bf16_pieces(y, 3)
-        upper, lower = jnp.concatenate([hi, mid], axis=0), jnp.concatenate([hi, lo], axis=0)
-        return dot(second[0], upper) + dot(second[1], upper) + dot(second[2], lower)
-
-    def add(k_re, k_im, weight):
+    def inward(at, pair, k):
+        k_re, k_im = kernels[at, k, 0], kernels[at, k, 1]
         re, im = spec_re[...], spec_im[...]
         product = jnp.concatenate([k_re * re - k_im * im, k_re * im + k_im * re], axis=0)
         hi, mid, lo = bf16_pieces(product, 3)
         upper, lower = jnp.concatenate([hi, mid], axis=1), jnp.concatenate([hi, lo], axis=1)
         inner = dot(upper, first[0]) + dot(upper, first[1]) + dot(lower, first[2])
         a, c, d, b = inner[:half, :half], inner[:half, half:], inner[half:, :half], inner[half:, half:]
-        y_re = jnp.concatenate([a - b, a + b], axis=1)
-        y_im = jnp.concatenate([c + d, d - c], axis=1)
-        of_re, of_im = outer(y_re), outer(y_im)
+        for slot, y in zip(pair, ((a - b, a + b), (c + d, d - c))):
+            for side, part in enumerate(y):
+                at_side = slice(side * half, (side + 1) * half)
+                hi, mid, lo = bf16_pieces(part, 3)
+                slot[0, :half, at_side] = hi
+                slot[0, half:, at_side] = mid
+                slot[1, :half, at_side] = hi
+                slot[1, half:, at_side] = lo
+
+    def outward(pair, weight):
+        of_re, of_im = (
+            dot(second[0], slot[0]) + dot(second[1], slot[0]) + dot(second[2], slot[1]) for slot in pair
+        )
         a, c, d, b = of_re[:half], of_re[half:], of_im[:half], of_im[half:]
         p_re, p_im, m_re, m_im = a - b, c + d, a + b, d - c
         plus[...] += weight * (p_re * p_re + p_im * p_im)
         minus[...] += weight * (m_re * m_re + m_im * m_im)
 
-    @pl.loop(0, spectra.shape[0])
-    def _(k):
-        add(kernels[0, k, 0], kernels[0, k, 1], my_weights[pl.ds(k, 1), :])
-        add(kernels[1, k, 0], kernels[1, k, 1], other_weights[pl.ds(k, 1), :])
+    last = spectra.shape[0] - 1
+    inward(0, slots[0], 0)
+    inward(1, slots[1], 0)
+
+    @pl.loop(0, spectra.shape[0] // 2)
+    def _(i):
+        k = 2 * i
+        following = jnp.minimum(k + 2, last)
+        outward(slots[0], my_weights[pl.ds(k, 1), :])
+        inward(0, slots[2], k + 1)
+        outward(slots[1], other_weights[pl.ds(k, 1), :])
+        inward(1, slots[3], k + 1)
+        outward(slots[2], my_weights[pl.ds(k + 1, 1), :])
+        inward(0, slots[0], following)
+        outward(slots[3], other_weights[pl.ds(k + 1, 1), :])
+        inward(1, slots[1], following)
 
     both = jnp.concatenate([exact(flip[...], minus[...]), plus[...]], axis=0)
     picture = jnp.concatenate([exact(both[:, half:], flip[...]), both[:, :half]], axis=1)
@@ -285,11 +298,14 @@
         return copies
 
     near_peers = [(d, near_peer(d)) for d in range(1, n_near)]
-    far_peers = [(d, far_peer(d)) for d in range(1, n_tx)]
+
+    @pl.when(has_up)
+    def _():
+        pl.semaphore_wait(token, 1)
 
     @pl.when(has_down)
     def _():
-        pl.semaphore_wait(ready, n_tx - 1 - tx)
+        pl.semaphore_signal(token, inc=1, device_id={"tx": tx + 1}, device_id_type=MESH)
 
     copies = swapped(near, place, near_peers, near_send, near_recv)
     of_iteration = []
@@ -299,9 +315,30 @@
             jnp.where(is_peak, functools.reduce(jnp.maximum, found_t), functools.reduce(jnp.add, found_t))
         )
     far[tx] = jnp.where((lane & 32) == 0, of_iteration[0], of_iteration[1])
-    far_copies = [small(far, tx, d, peer, far_send, far_recv) for d, (_, peer) in far_peers]
-    for copy in far_copies:
-        copy.start()
+
+    def far_copy(d, up):
+        spot = tx - d if up else tx + d
+        return small(far, tx, d - 1 if up else n_tx - 1 + d - 1, {"tx": spot}, far_send, far_recv)
+
+    for d in range(1, n_tx):
+        @pl.when(tx - d >= 0)
+        def _():
+            far_copy(d, True).start()
+
+    for d in range(1, n_tx):
+        @pl.when(tx - d >= 0)
+        def _():
+            pl.semaphore_signal(ready, inc=1, device_id={"tx": tx - d}, device_id_type=MESH)
+
+    @pl.when(has_down)
+    def _():
+        pl.semaphore_wait(ready, n_tx - 1 - tx)
+
+    for d in range(1, n_tx):
+        @pl.when(tx + d < n_tx)
+        def _():
+            far_copy(d, False).start()
+
     send_errors.start()
     send_image.wait()
     send_errors.wait()
@@ -316,19 +353,21 @@
     pl.when(has_right)(to_right.wait_send)
     for copy in copies:
         copy.wait_send()
-    for d, (spot, peer) in far_peers:
-        small(far, spot, d, peer, far_send, far_recv).wait_recv()
+    for d in range(1, n_tx):
+        spot, peer = far_peer(d)
+        small(far, spot, 0, peer, far_send, far_recv).wait_recv()
     stats_out[...] = jnp.where(is_peak, jnp.max(far[...], axis=0), jnp.sum(far[...], axis=0))
     saves[3].start()
-    for copy in far_copies:
-        copy.wait_send()
+    for d in range(1, n_tx):
+        for up in (True, False):
+            pl.when(tx - d >= 0 if up else tx + d < n_tx)(far_copy(d, up).wait_send)
     for save in saves:
         save.wait()
 
 
 def deliver_kernel(
     n_sites, image, mask, errors, stats, intensity, new_mask, edge_errors, peaks, shares,
-    image_at, mask_at, errors_at, stats_at, sem,
+    image_at, mask_at, errors_at, stats_at, peaks_at, shares_at, sem,
 ):
     held = ((stats, stats_at, None), (image, image_at, intensity), (mask, mask_at, new_mask), (errors, errors_at, edge_errors))
     loads = [pltpu.make_async_copy(src, at, sem.at[0, i]) for i, (src, at, _) in enumerate(held)]
@@ -336,13 +375,17 @@
     for load in loads:
         load.start()
     loads[0].wait()
+    final = stats_at[...]
+    for t in range(ITERS):
+        peaks_at[t] = final[0, 32 * t]
+        shares_at[t] = final[0, 64 + 32 * t] * (1.0 / n_sites)
+    pairs = ((peaks_at, peaks), (shares_at, shares))
+    copies += [pltpu.make_async_copy(at, dst, sem.at[1, 4 * i]) for i, (at, dst) in enumerate(pairs)]
+    for copy in copies[3:]:
+        copy.start()
     for load, copy in zip(loads[1:], copies):
         load.wait()
         copy.start()
-    final = stats_at[...]
-    for t in range(ITERS):
-        peaks[t] = final[0, 32 * t]
-        shares[t] = final[0, 64 + 32 * t] * (1.0 / n_sites)
     for copy in copies:
         copy.wait()
 
@@ -359,7 +402,6 @@
     n_near = lax.axis_size("ty") * lax.axis_size("ka")
     n_tx = lax.axis_size("tx")
     constants = [jnp.asarray(t) for t in tables(tile)]
-    smem = pl.BlockSpec(memory_space=pltpu.SMEM)
     hbm = pl.BlockSpec(memory_space=pltpu.HBM)
     dma = pltpu.SemaphoreType.DMA
     errors_shape = jax.ShapeDtypeStruct((1, 1, ITERS, n_sites), f32)
@@ -382,8 +424,8 @@
             V((half, tile), f32), V((half, tile), f32), V((tile, tile), f32), V((tile, tile), f32),
             V((1, n_sites), f32), V((1, n_sites), f32), V((n_near, 1, 128), f32), V((n_tx, 1, 128), f32),
             V((tile, tile), f32), V((tile, tile), f32), V(errors_shape.shape, f32), V((1, 128), f32),
-            dma((17,)), dma((4,)), dma((6,)), dma((6,)), dma((n_near + 2,)), dma((n_near + 2,)), dma((n_tx,)), dma((n_tx,)),
-            pltpu.SemaphoreType.REGULAR,
+            *([V((2, tile, tile), bf16)] * 8), dma((17,)), dma((4,)), dma((6,)), dma((6,)), dma((n_near + 2,)), dma((n_near + 2,)), dma((2 * n_tx,)), dma((n_tx,)),
+            pltpu.SemaphoreType.REGULAR, pltpu.SemaphoreType.REGULAR,
         ],
         compiler_params=pltpu.CompilerParams(collective_id=0, has_side_effects=True),
         cost_estimate=pl.CostEstimate(flops=4 * 10**9, bytes_accessed=4 * 10**6, transcendentals=0),
@@ -397,9 +439,10 @@
         name="deliver_kernel",
         out_shape=(square, square, errors_shape, pair, pair),
         in_specs=[hbm] * 4,
-        out_specs=(hbm, hbm, hbm, smem, smem),
+        out_specs=(hbm,) * 5,
         scratch_shapes=[
-            V((tile, tile), f32), V((tile, tile), f32), V(errors_shape.shape, f32), V((1, 128), f32), dma((2, 4)),
+            V((tile, tile), f32), V((tile, tile), f32), V(errors_shape.shape, f32), V((1, 128), f32),
+            pltpu.SMEM((ITERS,), f32), pltpu.SMEM((ITERS,), f32), dma((2, 5)),
         ],
     )(image, new_mask, errors, stats)
 

time: 60.2 us -> 68.3 us (1.13)
  Pallas kernels: 59.4 us -> 67.5 us
    pallas_call x1, Pallas kernels: 57.1 us -> 65.7 us  [shards(): pl.pallas_call(opc_kernel, name='opc_kernel', out_shape=(square, square,...]
where the time goes in v2:
time: 68.3 us; the launch traced here: 68.2 us
  Pallas kernels  67.5 us (99%)
    pallas_call x1, Pallas kernels, shards(): pl.pallas_call(opc_kernel, name='opc_kernel', out_shape=(square, square,...  65.7 us
    pallas_call x1, Pallas kernels, shards(): pl.pallas_call(functools.partial(deliver_kernel, float(n_sites * n_tx * l...  1.85 us

profile of v2, /device:TPU:33, one launch (start us, length us, event | category | flops | bytes accessed | tf_op | source)
XLA Modules:
  0.0 68.2 jit_solution(16553240539423963860)
XLA Ops:
  0.6 65.7 %opc_kernel.1 = (f32[256,256]{1,0:T(8,128)}, f32[256,256]{1,0:T(8,128)}, f32[1,1,2,2048]{3,2,1,0:T(2,128)}, f32[1,128]{1,0:T(1,128)}) custom-call(f32[256,256]{1,0:T(8,128)} %mask.1, s32[1,1,512]{2,1,0:T(1,128)} %rows_at.1, s32[1,1,512]{2,1,0:T(1,128)} %cols_at.1, s32[1,1,512]{2,1,0:T(1,128)} %lengths.1, s32[1,1,512]{2,1,0:T(1,128)} %orients.1, ...), custom_call_target="tpu_custom_call" | custom-call | flops 4000000000 | bytes 4000000 | tf_op jit(solution)/shard_map/opc_kernel/pallas_call | solution.py:410
  66.3 1.9 %deliver_kernel.1 = (f32[256,256]{1,0:T(8,128)}, f32[256,256]{1,0:T(8,128)}, f32[1,1,2,2048]{3,2,1,0:T(2,128)}, f32[2]{0:T(128)}, f32[2]{0:T(128)}) custom-call(f32[256,256]{1,0:T(8,128)} %get-tuple-element.9.image, f32[256,256]{1,0:T(8,128)} %get-tuple-element.10.mask, f32[1,1,2,2048]{3,2,1,0:T(2,128)} %get-tuple-element.11.errors, ...), custom_call_target="tpu_custom_call" | custom-call | tf_op jit(solution)/shard_map/deliver_kernel/pallas_call | solution.py:437

commit v3 on v2

--- a/solution.py
+++ b/solution.py
@@ -80,7 +80,7 @@
     row_dft, col_dft, expand, first, second, flip,
     above, below, packed, left, right, spec_re, spec_im, wanted,
     plus, minus, image, image_in, errors, errors_in, near, far, mask_out, image_out, errors_out, stats_out,
-    slot_a, slot_b, slot_c, slot_d, slot_e, slot_f, slot_g, slot_h, load_sem, save_sem, halo_send, halo_recv, near_send, near_recv, far_send, far_recv, token, ready,
+    slot_a, slot_b, slot_c, slot_d, slot_e, slot_f, slot_g, slot_h, load_sem, save_sem, halo_send, halo_recv, near_send, near_recv, far_send, far_recv, ready,
 ):
     tx, ty, ka = lax.axis_index("tx"), lax.axis_index("ty"), lax.axis_index("ka")
     n_tx, n_ty, n_ka = lax.axis_size("tx"), lax.axis_size("ty"), lax.axis_size("ka")
@@ -119,9 +119,10 @@
     def _():
         pl.semaphore_signal(barrier, inc=1, device_id={"tx": tx - 1}, device_id_type=MESH)
 
-    @pl.when(has_down)
-    def _():
-        pl.semaphore_signal(barrier, inc=1, device_id={"tx": tx + 1}, device_id_type=MESH)
+    for d in range(1, n_tx):
+        @pl.when(tx + d < n_tx)
+        def _():
+            pl.semaphore_signal(barrier, inc=1, device_id={"tx": tx + d}, device_id_type=MESH)
 
     for load in loads[:7]:
         load.wait()
@@ -149,7 +150,7 @@
     for k in range(my_weights.shape[0]):
         my_weights[pl.ds(k, 1), :] = jnp.full((1, my_weights.shape[1]), weight_of[k], jnp.float32)
 
-    pl.semaphore_wait(barrier, n_near - 1 + has_up.astype(jnp.int32) + has_down.astype(jnp.int32))
+    pl.semaphore_wait(barrier, n_near - 1 + tx + has_down.astype(jnp.int32))
 
     def hop(source, target, number, device):
         return pltpu.make_async_remote_copy(
@@ -170,6 +171,11 @@
     pairs = ((mask_out, new_mask), (image_out, intensity), (errors_out, edge_errors), (stats_out, stats))
     saves = [pltpu.make_async_copy(src, dst, save_sem.at[i]) for i, (src, dst) in enumerate(pairs)]
     saves[0].start()
+    for d in range(1, n_tx):
+        @pl.when(tx - d >= 0)
+        def _():
+            pl.semaphore_signal(ready, inc=1, device_id={"tx": tx - d}, device_id_type=MESH)
+
     def arrived(there, copy, buffer):
         pl.when(there)(copy.wait_recv)
 
@@ -299,13 +305,9 @@
 
     near_peers = [(d, near_peer(d)) for d in range(1, n_near)]
 
-    @pl.when(has_up)
-    def _():
-        pl.semaphore_wait(token, 1)
-
     @pl.when(has_down)
     def _():
-        pl.semaphore_signal(token, inc=1, device_id={"tx": tx + 1}, device_id_type=MESH)
+        pl.semaphore_wait(ready, n_tx - 1 - tx)
 
     copies = swapped(near, place, near_peers, near_send, near_recv)
     of_iteration = []
@@ -315,30 +317,9 @@
             jnp.where(is_peak, functools.reduce(jnp.maximum, found_t), functools.reduce(jnp.add, found_t))
         )
     far[tx] = jnp.where((lane & 32) == 0, of_iteration[0], of_iteration[1])
-
-    def far_copy(d, up):
-        spot = tx - d if up else tx + d
-        return small(far, tx, d - 1 if up else n_tx - 1 + d - 1, {"tx": spot}, far_send, far_recv)
-
-    for d in range(1, n_tx):
-        @pl.when(tx - d >= 0)
-        def _():
-            far_copy(d, True).start()
-
-    for d in range(1, n_tx):
-        @pl.when(tx - d >= 0)
-        def _():
-            pl.semaphore_signal(ready, inc=1, device_id={"tx": tx - d}, device_id_type=MESH)
-
-    @pl.when(has_down)
-    def _():
-        pl.semaphore_wait(ready, n_tx - 1 - tx)
-
-    for d in range(1, n_tx):
-        @pl.when(tx + d < n_tx)
-        def _():
-            far_copy(d, False).start()
-
+    far_copies = [small(far, tx, d, far_peer(d)[1], far_send, far_recv) for d in range(1, n_tx)]
+    for copy in far_copies:
+        copy.start()
     send_errors.start()
     send_image.wait()
     send_errors.wait()
@@ -358,9 +339,8 @@
         small(far, spot, 0, peer, far_send, far_recv).wait_recv()
     stats_out[...] = jnp.where(is_peak, jnp.max(far[...], axis=0), jnp.sum(far[...], axis=0))
     saves[3].start()
-    for d in range(1, n_tx):
-        for up in (True, False):
-            pl.when(tx - d >= 0 if up else tx + d < n_tx)(far_copy(d, up).wait_send)
+    for copy in far_copies:
+        copy.wait_send()
     for save in saves:
         save.wait()
 
@@ -424,8 +404,8 @@
             V((half, tile), f32), V((half, tile), f32), V((tile, tile), f32), V((tile, tile), f32),
             V((1, n_sites), f32), V((1, n_sites), f32), V((n_near, 1, 128), f32), V((n_tx, 1, 128), f32),
             V((tile, tile), f32), V((tile, tile), f32), V(errors_shape.shape, f32), V((1, 128), f32),
-            *([V((2, tile, tile), bf16)] * 8), dma((17,)), dma((4,)), dma((6,)), dma((6,)), dma((n_near + 2,)), dma((n_near + 2,)), dma((2 * n_tx,)), dma((n_tx,)),
-            pltpu.SemaphoreType.REGULAR, pltpu.SemaphoreType.REGULAR,
+            *([V((2, tile, tile), bf16)] * 8), dma((17,)), dma((4,)), dma((6,)), dma((6,)), dma((n_near + 2,)), dma((n_near + 2,)), dma((n_tx,)), dma((n_tx,)),
+            pltpu.SemaphoreType.REGULAR,
         ],
         compiler_params=pltpu.CompilerParams(collective_id=0, has_side_effects=True),
         cost_estimate=pl.CostEstimate(flops=4 * 10**9, bytes_accessed=4 * 10**6, transcendentals=0),

time: 68.3 us -> 56.3 us (0.82)
  Pallas kernels: 67.5 us -> 55.5 us
    pallas_call x1, Pallas kernels: 65.7 us -> 53.7 us  [shards(): pl.pallas_call(opc_kernel, name='opc_kernel', out_shape=(square, square,...]
where the time goes in v3:
time: 56.3 us; the launch traced here: 56.2 us
  Pallas kernels  55.5 us (99%)
  between operations  0.64 us (1%)
    pallas_call x1, Pallas kernels, shards(): pl.pallas_call(opc_kernel, name='opc_kernel', out_shape=(square, square,...  53.7 us
    pallas_call x1, Pallas kernels, shards(): pl.pallas_call(functools.partial(deliver_kernel, float(n_sites * n_tx * l...  1.85 us

profile of v3, /device:TPU:33, one launch (start us, length us, event | category | flops | bytes accessed | tf_op | source)
XLA Modules:
  0.0 56.2 jit_solution(1116746105328178969)
XLA Ops:
  0.6 53.7 %opc_kernel.1 = (f32[256,256]{1,0:T(8,128)}, f32[256,256]{1,0:T(8,128)}, f32[1,1,2,2048]{3,2,1,0:T(2,128)}, f32[1,128]{1,0:T(1,128)}) custom-call(f32[256,256]{1,0:T(8,128)} %mask.1, s32[1,1,512]{2,1,0:T(1,128)} %rows_at.1, s32[1,1,512]{2,1,0:T(1,128)} %cols_at.1, s32[1,1,512]{2,1,0:T(1,128)} %lengths.1, s32[1,1,512]{2,1,0:T(1,128)} %orients.1, ...), custom_call_target="tpu_custom_call" | custom-call | flops 4000000000 | bytes 4000000 | tf_op jit(solution)/shard_map/opc_kernel/pallas_call | solution.py:390
  54.3 1.9 %deliver_kernel.1 = (f32[256,256]{1,0:T(8,128)}, f32[256,256]{1,0:T(8,128)}, f32[1,1,2,2048]{3,2,1,0:T(2,128)}, f32[2]{0:T(128)}, f32[2]{0:T(128)}) custom-call(f32[256,256]{1,0:T(8,128)} %get-tuple-element.9.image, f32[256,256]{1,0:T(8,128)} %get-tuple-element.10.mask, f32[1,1,2,2048]{3,2,1,0:T(2,128)} %get-tuple-element.11.errors, ...), custom_call_target="tpu_custom_call" | custom-call | tf_op jit(solution)/shard_map/deliver_kernel/pallas_call | solution.py:417

commit v4 on v3

--- a/solution.py
+++ b/solution.py
@@ -15,10 +15,9 @@
 LEVEL = 0.4
 SLOPE_FLOOR = 0.05
 SHARPNESS = 8.0
-HIGHEST = lax.Precision.HIGHEST
 MESH = pl.DeviceIdType.MESH
 SIN_AT = 72
-PACKED = 136
+PACKED = 144
 
 
 def bf16_pieces(x, count):
@@ -43,12 +42,18 @@
     theta = 2.0 * math.pi / ext
     inside = np.arange(ext) - (ext - 1) / 2
     low = BAND // 2
+    order = np.roll(np.arange(ext), -HALO)
+    order = np.concatenate([order[:tile], order[-HALO:], order[tile:-HALO]])
+    inside = inside[order]
     rows = np.zeros((PACKED, ext))
     rows[: low + 1] = np.cos(theta * np.outer(np.arange(low + 1), inside))
     rows[SIN_AT : SIN_AT + low] = np.sin(theta * np.outer(np.arange(1, low + 1), inside))
+    rows = np.concatenate(host_pieces(rows), axis=0)
+    rows = np.stack([rows[:, :tile], rows[:, tile:]])
     freq = np.arange(BAND) - low
     turns = theta * np.outer(inside, freq)
-    cols = np.concatenate([np.cos(turns), np.sin(turns)], axis=1)
+    cols = np.stack(host_pieces(np.concatenate([np.cos(turns), np.sin(turns)], axis=1)))
+    cols = np.stack([cols[:, :tile], cols[:, tile:]])
     expand = np.zeros((2 * BAND, PACKED))
     for u, f in enumerate(freq):
         expand[u, abs(f)] = 1.0
@@ -60,25 +65,39 @@
     first = np.stack([np.concatenate(b, axis=0) for b in ((hi, hi), (mid, mid), (lo, hi))])
     second = np.ascontiguousarray(first.swapaxes(1, 2))
     flip = np.eye(half)[::-1]
-    f32 = np.float32
-    return rows.astype(f32), cols.astype(f32), expand.astype(f32), first, second, flip.astype(f32)
-
-
-def exact(left, right):
-    return jnp.dot(left, right, precision=HIGHEST, preferred_element_type=jnp.float32)
+    flip = np.concatenate([flip, flip], axis=1)
+    bf16 = jnp.bfloat16
+    return rows, cols, expand.astype(bf16), first, second, flip.astype(bf16), flip.T.astype(bf16)
 
 
 def dot(left, right):
     return jnp.dot(left, right, preferred_element_type=jnp.float32)
 
 
+def pieces_sum(of_hi, of_mid, of_lo):
+    n = of_lo.shape[0]
+    return of_hi[:n] + ((of_mid[:n] + of_hi[n : 2 * n]) + ((of_lo + of_hi[2 * n :]) + of_mid[n:]))
+
+
+def rows_product(table, x):
+    n = PACKED
+    hi, mid, lo = bf16_pieces(x, 3)
+    return pieces_sum(dot(table[...], hi), dot(table[: 2 * n], mid), dot(table[:n], lo))
+
+
+def cols_product(x, table):
+    n = PACKED
+    pieces = jnp.concatenate(bf16_pieces(x, 3), axis=0)
+    return pieces_sum(dot(pieces, table[0]), dot(pieces[: 2 * n], table[1]), dot(pieces[:n], table[2]))
+
+
 def opc_kernel(
     mask, rows_at, cols_at, lengths, orients, moves, site_rows, site_cols, spectra, weights, tolerance,
-    row_dft_in, col_dft_in, expand_in, first_in, second_in, flip_in,
+    row_dft_in, col_dft_in, expand_in, first_in, second_in, flip_rows_in, flip_cols_in,
     new_mask, intensity, edge_errors, stats,
     current, fragments, frag_moves, sites, kernels, my_weights, other_weights, weight_of, limits,
-    row_dft, col_dft, expand, first, second, flip,
-    above, below, packed, left, right, spec_re, spec_im, wanted,
+    row_dft, col_dft, expand, first, second, flip_rows, flip_cols,
+    halo_rows, packed, halo_cols, sums, spec_re, spec_im, wanted,
     plus, minus, image, image_in, errors, errors_in, near, far, mask_out, image_out, errors_out, stats_out,
     slot_a, slot_b, slot_c, slot_d, slot_e, slot_f, slot_g, slot_h, load_sem, save_sem, halo_send, halo_recv, near_send, near_recv, far_send, far_recv, ready,
 ):
@@ -97,7 +116,8 @@
         (mask, current), (rows_at, fragments.at[0]), (cols_at, fragments.at[1]), (lengths, fragments.at[2]),
         (orients, fragments.at[3]), (moves, frag_moves), (weights, weight_of), (row_dft_in, row_dft),
         (site_cols, sites.at[0]), (col_dft_in, col_dft), (expand_in, expand), (spectra, kernels.at[0]),
-        (first_in, first), (second_in, second), (flip_in, flip), (site_rows, sites.at[1]), (tolerance, limits),
+        (first_in, first), (second_in, second), (flip_rows_in, flip_rows), (flip_cols_in, flip_cols),
+        (site_rows, sites.at[1]), (tolerance, limits),
     ]
     loads = [pltpu.make_async_copy(src, dst, load_sem.at[i]) for i, (src, dst) in enumerate(pairs)]
     for load in loads:
@@ -158,6 +178,8 @@
             device_id=device, device_id_type=MESH,
         )
 
+    above, below = halo_rows.at[pl.ds(0, HALO)], halo_rows.at[pl.ds(HALO, HALO)]
+    left, right = halo_cols.at[:, pl.ds(0, HALO)], halo_cols.at[:, pl.ds(HALO, HALO)]
     to_up = hop(current.at[pl.ds(0, half)], below, 0, {"tx": tx - 1})
     to_down = hop(current.at[pl.ds(half, half)], above, 1, {"tx": tx + 1})
     to_left = hop(packed.at[:, pl.ds(0, half)], right, 2, {"ty": ty - 1})
@@ -184,7 +206,7 @@
             buffer[...] = jnp.zeros_like(buffer)
 
     loads[7].wait()
-    part = exact(row_dft[:, HALO : HALO + tile], current[...])
+    packed[...] = rows_product(row_dft.at[0], current[...])
     loads[8].wait()
     place_at = lax.broadcasted_iota(jnp.int32, (tile, tile), 0)
     chunks = site_rows.shape[2] // tile
@@ -195,19 +217,18 @@
         load.wait()
     arrived(has_up, to_down, above)
     arrived(has_down, to_up, below)
-    part = part + exact(row_dft[:, :HALO], above[...]) + exact(row_dft[:, HALO + tile :], below[...])
-    packed[...] = part
+    packed[...] += rows_product(row_dft.at[1], halo_rows[...])
     pl.when(has_left)(to_left.start)
     pl.when(has_right)(to_right.start)
-    sums = exact(part, col_dft[HALO : HALO + tile, :])
+    sums[...] = cols_product(packed[...], col_dft.at[0])
     plus[...] = jnp.zeros_like(plus)
     minus[...] = jnp.zeros_like(minus)
     swap_weights.wait()
     swap_spectra.wait()
     arrived(has_left, to_right, left)
     arrived(has_right, to_left, right)
-    sums = sums + exact(left[...], col_dft[:HALO, :]) + exact(right[...], col_dft[HALO + tile :, :])
-    full = exact(expand[...], sums)
+    total = sums[...] + cols_product(halo_cols[...], col_dft.at[1])
+    full = sum(dot(expand[...], piece) for piece in bf16_pieces(total, 3))
     scale = 1.0 / (ext * ext)
     spec_re[...] = (full[:BAND, :BAND] - full[BAND:, BAND:]) * scale
     spec_im[...] = (full[BAND:, :BAND] + full[:BAND, BAND:]) * -scale
@@ -255,8 +276,12 @@
         outward(slots[3], other_weights[pl.ds(k + 1, 1), :])
         inward(1, slots[1], following)
 
-    both = jnp.concatenate([exact(flip[...], minus[...]), plus[...]], axis=0)
-    picture = jnp.concatenate([exact(both[:, half:], flip[...]), both[:, :half]], axis=1)
+    hi, mid, lo = bf16_pieces(minus[...], 3)
+    turned = dot(flip_rows[...], jnp.concatenate([hi, mid], axis=0)) + dot(flip_rows[:, :half], lo)
+    both = jnp.concatenate([turned, plus[...]], axis=0)
+    hi, mid, lo = bf16_pieces(both[:, half:], 3)
+    turned = dot(jnp.concatenate([hi, mid], axis=1), flip_cols[...]) + dot(lo, flip_cols[:half])
+    picture = jnp.concatenate([turned, both[:, :half]], axis=1)
     image[...] = picture
     grad_rows = (pltpu.roll(picture, tile - 1, 0) - pltpu.roll(picture, 1, 0)) * 0.5
     grad_cols = (pltpu.roll(picture, tile - 1, 1) - pltpu.roll(picture, 1, 1)) * 0.5
@@ -391,20 +416,20 @@
         opc_kernel,
         name="opc_kernel",
         out_shape=(square, square, errors_shape, jax.ShapeDtypeStruct((1, 128), f32)),
-        in_specs=[hbm] * 17,
+        in_specs=[hbm] * 18,
         out_specs=(hbm,) * 4,
         scratch_shapes=[
             V((tile, tile), f32), V((4, *frag_rows.shape), i32), V(frag_moves.shape, i32),
             V((2, *site_rows.shape), i32), V((2, *spectra.shape), f32), V((kernels, tile), f32),
             V((kernels, tile), f32), pltpu.SMEM(weights.shape, f32), pltpu.SMEM(tolerance.shape, i32),
             *(V(c.shape, c.dtype) for c in constants),
-            V((HALO, tile), f32), V((HALO, tile), f32), V((PACKED, tile), f32),
-            V((PACKED, HALO), f32), V((PACKED, HALO), f32), V((BAND, BAND), f32), V((BAND, BAND), f32),
+            V((2 * HALO, tile), f32), V((PACKED, tile), f32), V((PACKED, 2 * HALO), f32), V((PACKED, 2 * BAND), f32),
+            V((BAND, BAND), f32), V((BAND, BAND), f32),
             V((tile, n_sites), bf16),
             V((half, tile), f32), V((half, tile), f32), V((tile, tile), f32), V((tile, tile), f32),
             V((1, n_sites), f32), V((1, n_sites), f32), V((n_near, 1, 128), f32), V((n_tx, 1, 128), f32),
             V((tile, tile), f32), V((tile, tile), f32), V(errors_shape.shape, f32), V((1, 128), f32),
-            *([V((2, tile, tile), bf16)] * 8), dma((17,)), dma((4,)), dma((6,)), dma((6,)), dma((n_near + 2,)), dma((n_near + 2,)), dma((n_tx,)), dma((n_tx,)),
+            *([V((2, tile, tile), bf16)] * 8), dma((18,)), dma((4,)), dma((6,)), dma((6,)), dma((n_near + 2,)), dma((n_near + 2,)), dma((n_tx,)), dma((n_tx,)),
             pltpu.SemaphoreType.REGULAR,
         ],
         compiler_params=pltpu.CompilerParams(collective_id=0, has_side_effects=True),

time: 56.3 us -> 55.1 us (0.979)
  Pallas kernels: 55.5 us -> 54.3 us
    pallas_call x1, Pallas kernels: 53.7 us -> 52.4 us  [shards(): pl.pallas_call(opc_kernel, name='opc_kernel', out_shape=(square, square,...]
where the time goes in v4:
time: 55.1 us; the launch traced here: 54.9 us
  Pallas kernels  54.3 us (99%)
  between operations  0.64 us (1%)
    pallas_call x1, Pallas kernels, shards(): pl.pallas_call(opc_kernel, name='opc_kernel', out_shape=(square, square,...  52.4 us
    pallas_call x1, Pallas kernels, shards(): pl.pallas_call(functools.partial(deliver_kernel, float(n_sites * n_tx * l...  1.85 us

profile of v4, /device:TPU:33, one launch (start us, length us, event | category | flops | bytes accessed | tf_op | source)
XLA Modules:
  0.0 54.9 jit_solution(12607940763115086479)
XLA Ops:
  0.6 52.4 %opc_kernel.1 = (f32[256,256]{1,0:T(8,128)}, f32[256,256]{1,0:T(8,128)}, f32[1,1,2,2048]{3,2,1,0:T(2,128)}, f32[1,128]{1,0:T(1,128)}) custom-call(f32[256,256]{1,0:T(8,128)} %mask.1, s32[1,1,512]{2,1,0:T(1,128)} %rows_at.1, s32[1,1,512]{2,1,0:T(1,128)} %cols_at.1, s32[1,1,512]{2,1,0:T(1,128)} %lengths.1, s32[1,1,512]{2,1,0:T(1,128)} %orients.1, ...), custom_call_target="tpu_custom_call" | custom-call | flops 4000000000 | bytes 4000000 | tf_op jit(solution)/shard_map/opc_kernel/pallas_call | solution.py:415
  53.1 1.9 %deliver_kernel.1 = (f32[256,256]{1,0:T(8,128)}, f32[256,256]{1,0:T(8,128)}, f32[1,1,2,2048]{3,2,1,0:T(2,128)}, f32[2]{0:T(128)}, f32[2]{0:T(128)}) custom-call(f32[256,256]{1,0:T(8,128)} %get-tuple-element.9.image, f32[256,256]{1,0:T(8,128)} %get-tuple-element.10.mask, f32[1,1,2,2048]{3,2,1,0:T(2,128)} %get-tuple-element.11.errors, ...), custom_call_target="tpu_custom_call" | custom-call | tf_op jit(solution)/shard_map/deliver_kernel/pallas_call | solution.py:442

commit v5 on v4

--- a/solution.py
+++ b/solution.py
@@ -99,7 +99,7 @@
     row_dft, col_dft, expand, first, second, flip_rows, flip_cols,
     halo_rows, packed, halo_cols, sums, spec_re, spec_im, wanted,
     plus, minus, image, image_in, errors, errors_in, near, far, mask_out, image_out, errors_out, stats_out,
-    slot_a, slot_b, slot_c, slot_d, slot_e, slot_f, slot_g, slot_h, load_sem, save_sem, halo_send, halo_recv, near_send, near_recv, far_send, far_recv, ready,
+    slot_a, slot_b, slot_c, slot_d, slot_e, slot_f, slot_g, slot_h, load_sem, save_sem, halo_send, halo_recv, near_send, near_recv, far_send, far_recv, relay_out, relay_in, relay_send, relay_recv, ready,
 ):
     tx, ty, ka = lax.axis_index("tx"), lax.axis_index("ty"), lax.axis_index("ka")
     n_tx, n_ty, n_ka = lax.axis_size("tx"), lax.axis_size("ty"), lax.axis_size("ka")
@@ -127,9 +127,10 @@
         spot = lax.rem(place + d, n_near)
         return spot, {"ty": spot // n_ka, "ka": lax.rem(spot, n_ka)}
 
-    def far_peer(d):
-        spot = lax.rem(tx + d, n_tx)
-        return spot, {"tx": spot}
+    reach = n_tx // 4
+    far_spots = [lax.rem(tx + d, n_tx) for d in (*range(1, reach + 1), *range(n_tx - reach, n_tx))]
+    below_me = [spot < tx for spot in far_spots]
+    n_below = sum(lower.astype(jnp.int32) for lower in below_me)
 
     barrier = pltpu.get_barrier_semaphore()
     for d in range(1, n_near):
@@ -139,10 +140,10 @@
     def _():
         pl.semaphore_signal(barrier, inc=1, device_id={"tx": tx - 1}, device_id_type=MESH)
 
-    for d in range(1, n_tx):
-        @pl.when(tx + d < n_tx)
+    for spot, lower in zip(far_spots, below_me):
+        @pl.when(jnp.logical_not(lower))
         def _():
-            pl.semaphore_signal(barrier, inc=1, device_id={"tx": tx + d}, device_id_type=MESH)
+            pl.semaphore_signal(barrier, inc=1, device_id={"tx": spot}, device_id_type=MESH)
 
     for load in loads[:7]:
         load.wait()
@@ -170,7 +171,7 @@
     for k in range(my_weights.shape[0]):
         my_weights[pl.ds(k, 1), :] = jnp.full((1, my_weights.shape[1]), weight_of[k], jnp.float32)
 
-    pl.semaphore_wait(barrier, n_near - 1 + tx + has_down.astype(jnp.int32))
+    pl.semaphore_wait(barrier, n_near - 1 + n_below + has_down.astype(jnp.int32))
 
     def hop(source, target, number, device):
         return pltpu.make_async_remote_copy(
@@ -193,10 +194,10 @@
     pairs = ((mask_out, new_mask), (image_out, intensity), (errors_out, edge_errors), (stats_out, stats))
     saves = [pltpu.make_async_copy(src, dst, save_sem.at[i]) for i, (src, dst) in enumerate(pairs)]
     saves[0].start()
-    for d in range(1, n_tx):
-        @pl.when(tx - d >= 0)
+    for spot, lower in zip(far_spots, below_me):
+        @pl.when(lower)
         def _():
-            pl.semaphore_signal(ready, inc=1, device_id={"tx": tx - d}, device_id_type=MESH)
+            pl.semaphore_signal(ready, inc=1, device_id={"tx": spot}, device_id_type=MESH)
 
     def arrived(there, copy, buffer):
         pl.when(there)(copy.wait_recv)
@@ -330,9 +331,9 @@
 
     near_peers = [(d, near_peer(d)) for d in range(1, n_near)]
 
-    @pl.when(has_down)
+    @pl.when(n_below < len(far_spots))
     def _():
-        pl.semaphore_wait(ready, n_tx - 1 - tx)
+        pl.semaphore_wait(ready, len(far_spots) - n_below)
 
     copies = swapped(near, place, near_peers, near_send, near_recv)
     of_iteration = []
@@ -342,7 +343,7 @@
             jnp.where(is_peak, functools.reduce(jnp.maximum, found_t), functools.reduce(jnp.add, found_t))
         )
     far[tx] = jnp.where((lane & 32) == 0, of_iteration[0], of_iteration[1])
-    far_copies = [small(far, tx, d, far_peer(d)[1], far_send, far_recv) for d in range(1, n_tx)]
+    far_copies = [small(far, tx, i, {"tx": spot}, far_send, far_recv) for i, spot in enumerate(far_spots)]
     for copy in far_copies:
         copy.start()
     send_errors.start()
@@ -359,12 +360,41 @@
     pl.when(has_right)(to_right.wait_send)
     for copy in copies:
         copy.wait_send()
-    for d in range(1, n_tx):
-        spot, peer = far_peer(d)
-        small(far, spot, 0, peer, far_send, far_recv).wait_recv()
-    stats_out[...] = jnp.where(is_peak, jnp.max(far[...], axis=0), jnp.sum(far[...], axis=0))
+
+    def combined(spots):
+        held = [far[spot] for spot in spots]
+        return jnp.where(is_peak, functools.reduce(jnp.maximum, held), functools.reduce(jnp.add, held))
+
+    def arrived_from(i):
+        small(far, far_spots[i], i, {"tx": far_spots[i]}, far_send, far_recv).wait_recv()
+
+    def relayed(side, spot):
+        return pltpu.make_async_remote_copy(
+            src_ref=relay_out.at[side], dst_ref=relay_in.at[side], send_sem=relay_send.at[side],
+            recv_sem=relay_recv.at[side], device_id={"tx": spot}, device_id_type=MESH,
+        )
+
+    for i in range(reach + 1, 2 * reach):
+        arrived_from(i)
+    relays = []
+    if reach > 1:
+        relay_out[0] = combined(far_spots[reach + 1 :])
+        relays.append(relayed(0, far_spots[reach - 1]))
+        relays[0].start()
+    for i in range(reach):
+        arrived_from(i)
+    relay_out[1] = combined(far_spots[:reach])
+    relays.append(relayed(1, far_spots[reach]))
+    relays[-1].start()
+    arrived_from(reach)
+    whole = [combined([*far_spots, tx])]
+    for copy in relays:
+        copy.wait_recv()
+    for side in ((0, 1) if reach > 1 else (1,)):
+        whole.append(relay_in[side])
+    stats_out[...] = jnp.where(is_peak, functools.reduce(jnp.maximum, whole), functools.reduce(jnp.add, whole))
     saves[3].start()
-    for copy in far_copies:
+    for copy in far_copies + relays:
         copy.wait_send()
     for save in saves:
         save.wait()
@@ -430,6 +460,7 @@
             V((1, n_sites), f32), V((1, n_sites), f32), V((n_near, 1, 128), f32), V((n_tx, 1, 128), f32),
             V((tile, tile), f32), V((tile, tile), f32), V(errors_shape.shape, f32), V((1, 128), f32),
             *([V((2, tile, tile), bf16)] * 8), dma((18,)), dma((4,)), dma((6,)), dma((6,)), dma((n_near + 2,)), dma((n_near + 2,)), dma((n_tx,)), dma((n_tx,)),
+            V((2, 1, 128), f32), V((2, 1, 128), f32), dma((2,)), dma((2,)),
             pltpu.SemaphoreType.REGULAR,
         ],
         compiler_params=pltpu.CompilerParams(collective_id=0, has_side_effects=True),

time: 55.1 us -> 55.3 us (level)
  the two profiles are of different devices: /device:TPU:33 before, /device:TPU:40 now
where the time goes in v5:
time: 55.3 us; the launch traced here: 55.1 us
  Pallas kernels  54.5 us (99%)
  between operations  0.64 us (1%)
    pallas_call x1, Pallas kernels, shards(): pl.pallas_call(opc_kernel, name='opc_kernel', out_shape=(square, square,...  52.6 us
    pallas_call x1, Pallas kernels, shards(): pl.pallas_call(functools.partial(deliver_kernel, float(n_sites * n_tx * l...  1.85 us

profile of v5, /device:TPU:40, one launch (start us, length us, event | category | flops | bytes accessed | tf_op | source)
XLA Modules:
  0.0 55.1 jit_solution(2348755324400979308)
XLA Ops:
  0.6 52.6 %opc_kernel.1 = (f32[256,256]{1,0:T(8,128)}, f32[256,256]{1,0:T(8,128)}, f32[1,1,2,2048]{3,2,1,0:T(2,128)}, f32[1,128]{1,0:T(1,128)}) custom-call(f32[256,256]{1,0:T(8,128)} %mask.1, s32[1,1,512]{2,1,0:T(1,128)} %rows_at.1, s32[1,1,512]{2,1,0:T(1,128)} %cols_at.1, s32[1,1,512]{2,1,0:T(1,128)} %lengths.1, s32[1,1,512]{2,1,0:T(1,128)} %orients.1, ...), custom_call_target="tpu_custom_call" | custom-call | flops 4000000000 | bytes 4000000 | tf_op jit(solution)/shard_map/opc_kernel/pallas_call | solution.py:445
  53.3 1.9 %deliver_kernel.1 = (f32[256,256]{1,0:T(8,128)}, f32[256,256]{1,0:T(8,128)}, f32[1,1,2,2048]{3,2,1,0:T(2,128)}, f32[2]{0:T(128)}, f32[2]{0:T(128)}) custom-call(f32[256,256]{1,0:T(8,128)} %get-tuple-element.9.image, f32[256,256]{1,0:T(8,128)} %get-tuple-element.10.mask, f32[1,1,2,2048]{3,2,1,0:T(2,128)} %get-tuple-element.11.errors, ...), custom_call_target="tpu_custom_call" | custom-call | tf_op jit(solution)/shard_map/deliver_kernel/pallas_call | solution.py:473

commit v6 on v5

--- a/solution.py
+++ b/solution.py
@@ -127,7 +127,9 @@
         spot = lax.rem(place + d, n_near)
         return spot, {"ty": spot // n_ka, "ka": lax.rem(spot, n_ka)}
 
-    reach = n_tx // 4
+    quarter = n_tx // 4
+    extra = max(quarter // 2, 1)
+    reach = 2 * quarter - extra
     far_spots = [lax.rem(tx + d, n_tx) for d in (*range(1, reach + 1), *range(n_tx - reach, n_tx))]
     below_me = [spot < tx for spot in far_spots]
     n_below = sum(lower.astype(jnp.int32) for lower in below_me)
@@ -374,23 +376,24 @@
             recv_sem=relay_recv.at[side], device_id={"tx": spot}, device_id_type=MESH,
         )
 
-    for i in range(reach + 1, 2 * reach):
-        arrived_from(i)
-    relays = []
-    if reach > 1:
-        relay_out[0] = combined(far_spots[reach + 1 :])
-        relays.append(relayed(0, far_spots[reach - 1]))
-        relays[0].start()
-    for i in range(reach):
-        arrived_from(i)
-    relay_out[1] = combined(far_spots[:reach])
-    relays.append(relayed(1, far_spots[reach]))
-    relays[-1].start()
-    arrived_from(reach)
+    from_above = list(range(quarter - extra, quarter))
+    from_below = [2 * reach - d for d in range(quarter - extra + 1, quarter)]
+    relays, sides = [], []
+    for side, chosen, to in ((0, from_above, 2 * reach - quarter), (1, from_below, quarter - 1)):
+        if chosen:
+            for i in chosen:
+                arrived_from(i)
+            relay_out[side] = combined([far_spots[i] for i in chosen])
+            relays.append(relayed(side, far_spots[to]))
+            relays[-1].start()
+            sides.append(side)
+    for i in range(2 * reach):
+        if i not in from_above + from_below:
+            arrived_from(i)
     whole = [combined([*far_spots, tx])]
     for copy in relays:
         copy.wait_recv()
-    for side in ((0, 1) if reach > 1 else (1,)):
+    for side in sides:
         whole.append(relay_in[side])
     stats_out[...] = jnp.where(is_peak, functools.reduce(jnp.maximum, whole), functools.reduce(jnp.add, whole))
     saves[3].start()

time: 55.3 us -> 56.9 us (1.029)
  the two profiles are of different devices: /device:TPU:40 before, /device:TPU:33 now
where the time goes in v6:
time: 56.9 us; the launch traced here: 55.8 us
  Pallas kernels  55.1 us (97%)
  between operations  0.64 us (1%)
    pallas_call x1, Pallas kernels, shards(): pl.pallas_call(opc_kernel, name='opc_kernel', out_shape=(square, square,...  53.3 us
    pallas_call x1, Pallas kernels, shards(): pl.pallas_call(functools.partial(deliver_kernel, float(n_sites * n_tx * l...  1.85 us

profile of v6, /device:TPU:33, one launch (start us, length us, event | category | flops | bytes accessed | tf_op | source)
XLA Modules:
  0.0 55.8 jit_solution(15204881627243980186)
XLA Ops:
  0.6 53.3 %opc_kernel.1 = (f32[256,256]{1,0:T(8,128)}, f32[256,256]{1,0:T(8,128)}, f32[1,1,2,2048]{3,2,1,0:T(2,128)}, f32[1,128]{1,0:T(1,128)}) custom-call(f32[256,256]{1,0:T(8,128)} %mask.1, s32[1,1,512]{2,1,0:T(1,128)} %rows_at.1, s32[1,1,512]{2,1,0:T(1,128)} %cols_at.1, s32[1,1,512]{2,1,0:T(1,128)} %lengths.1, s32[1,1,512]{2,1,0:T(1,128)} %orients.1, ...), custom_call_target="tpu_custom_call" | custom-call | flops 4000000000 | bytes 4000000 | tf_op jit(solution)/shard_map/opc_kernel/pallas_call | solution.py:448
  53.9 1.9 %deliver_kernel.1 = (f32[256,256]{1,0:T(8,128)}, f32[256,256]{1,0:T(8,128)}, f32[1,1,2,2048]{3,2,1,0:T(2,128)}, f32[2]{0:T(128)}, f32[2]{0:T(128)}) custom-call(f32[256,256]{1,0:T(8,128)} %get-tuple-element.9.image, f32[256,256]{1,0:T(8,128)} %get-tuple-element.10.mask, f32[1,1,2,2048]{3,2,1,0:T(2,128)} %get-tuple-element.11.errors, ...), custom_call_target="tpu_custom_call" | custom-call | tf_op jit(solution)/shard_map/deliver_kernel/pallas_call | solution.py:476

commit v7 on v6

--- a/solution.py
+++ b/solution.py
@@ -128,7 +128,7 @@
         return spot, {"ty": spot // n_ka, "ka": lax.rem(spot, n_ka)}
 
     quarter = n_tx // 4
-    extra = max(quarter // 2, 1)
+    extra = 1
     reach = 2 * quarter - extra
     far_spots = [lax.rem(tx + d, n_tx) for d in (*range(1, reach + 1), *range(n_tx - reach, n_tx))]
     below_me = [spot < tx for spot in far_spots]
@@ -270,14 +270,14 @@
     def _(i):
         k = 2 * i
         following = jnp.minimum(k + 2, last)
+        inward(0, slots[2], k + 1)
         outward(slots[0], my_weights[pl.ds(k, 1), :])
-        inward(0, slots[2], k + 1)
+        inward(1, slots[3], k + 1)
         outward(slots[1], other_weights[pl.ds(k, 1), :])
-        inward(1, slots[3], k + 1)
+        inward(0, slots[0], following)
         outward(slots[2], my_weights[pl.ds(k + 1, 1), :])
-        inward(0, slots[0], following)
+        inward(1, slots[1], following)
         outward(slots[3], other_weights[pl.ds(k + 1, 1), :])
-        inward(1, slots[1], following)
 
     hi, mid, lo = bf16_pieces(minus[...], 3)
     turned = dot(flip_rows[...], jnp.concatenate([hi, mid], axis=0)) + dot(flip_rows[:, :half], lo)

time: 56.9 us -> 56.7 us (level)
  no operation moved by 1% of the time
where the time goes in v7:
time: 56.7 us; the launch traced here: 56.1 us
  Pallas kernels  55.5 us (98%)
  between operations  0.64 us (1%)
    pallas_call x1, Pallas kernels, shards(): pl.pallas_call(opc_kernel, name='opc_kernel', out_shape=(square, square,...  53.6 us
    pallas_call x1, Pallas kernels, shards(): pl.pallas_call(functools.partial(deliver_kernel, float(n_sites * n_tx * l...  1.85 us

profile of v7, /device:TPU:33, one launch (start us, length us, event | category | flops | bytes accessed | tf_op | source)
XLA Modules:
  0.0 56.1 jit_solution(16882184282658680665)
XLA Ops:
  0.6 53.6 %opc_kernel.1 = (f32[256,256]{1,0:T(8,128)}, f32[256,256]{1,0:T(8,128)}, f32[1,1,2,2048]{3,2,1,0:T(2,128)}, f32[1,128]{1,0:T(1,128)}) custom-call(f32[256,256]{1,0:T(8,128)} %mask.1, s32[1,1,512]{2,1,0:T(1,128)} %rows_at.1, s32[1,1,512]{2,1,0:T(1,128)} %cols_at.1, s32[1,1,512]{2,1,0:T(1,128)} %lengths.1, s32[1,1,512]{2,1,0:T(1,128)} %orients.1, ...), custom_call_target="tpu_custom_call" | custom-call | flops 4000000000 | bytes 4000000 | tf_op jit(solution)/shard_map/opc_kernel/pallas_call | solution.py:448
  54.3 1.9 %deliver_kernel.1 = (f32[256,256]{1,0:T(8,128)}, f32[256,256]{1,0:T(8,128)}, f32[1,1,2,2048]{3,2,1,0:T(2,128)}, f32[2]{0:T(128)}, f32[2]{0:T(128)}) custom-call(f32[256,256]{1,0:T(8,128)} %get-tuple-element.9.image, f32[256,256]{1,0:T(8,128)} %get-tuple-element.10.mask, f32[1,1,2,2048]{3,2,1,0:T(2,128)} %get-tuple-element.11.errors, ...), custom_call_target="tpu_custom_call" | custom-call | tf_op jit(solution)/shard_map/deliver_kernel/pallas_call | solution.py:476

commit v8 on v4

--- a/solution.py
+++ b/solution.py
@@ -267,14 +267,14 @@
     def _(i):
         k = 2 * i
         following = jnp.minimum(k + 2, last)
+        inward(0, slots[2], k + 1)
         outward(slots[0], my_weights[pl.ds(k, 1), :])
-        inward(0, slots[2], k + 1)
+        inward(1, slots[3], k + 1)
         outward(slots[1], other_weights[pl.ds(k, 1), :])
-        inward(1, slots[3], k + 1)
+        inward(0, slots[0], following)
         outward(slots[2], my_weights[pl.ds(k + 1, 1), :])
-        inward(0, slots[0], following)
+        inward(1, slots[1], following)
         outward(slots[3], other_weights[pl.ds(k + 1, 1), :])
-        inward(1, slots[1], following)
 
     hi, mid, lo = bf16_pieces(minus[...], 3)
     turned = dot(flip_rows[...], jnp.concatenate([hi, mid], axis=0)) + dot(flip_rows[:, :half], lo)

time: 55.1 us -> 55 us (level)
  no operation moved by 1% of the time
where the time goes in v8:
time: 55 us; the launch traced here: 54.8 us
  Pallas kernels  54.2 us (99%)
  between operations  0.64 us (1%)
    pallas_call x1, Pallas kernels, shards(): pl.pallas_call(opc_kernel, name='opc_kernel', out_shape=(square, square,...  52.3 us
    pallas_call x1, Pallas kernels, shards(): pl.pallas_call(functools.partial(deliver_kernel, float(n_sites * n_tx * l...  1.85 us

profile of v8, /device:TPU:33, one launch (start us, length us, event | category | flops | bytes accessed | tf_op | source)
XLA Modules:
  0.0 54.8 jit_solution(1707341170111807893)
XLA Ops:
  0.6 52.3 %opc_kernel.1 = (f32[256,256]{1,0:T(8,128)}, f32[256,256]{1,0:T(8,128)}, f32[1,1,2,2048]{3,2,1,0:T(2,128)}, f32[1,128]{1,0:T(1,128)}) custom-call(f32[256,256]{1,0:T(8,128)} %mask.1, s32[1,1,512]{2,1,0:T(1,128)} %rows_at.1, s32[1,1,512]{2,1,0:T(1,128)} %cols_at.1, s32[1,1,512]{2,1,0:T(1,128)} %lengths.1, s32[1,1,512]{2,1,0:T(1,128)} %orients.1, ...), custom_call_target="tpu_custom_call" | custom-call | flops 4000000000 | bytes 4000000 | tf_op jit(solution)/shard_map/opc_kernel/pallas_call | solution.py:415
  53.0 1.9 %deliver_kernel.1 = (f32[256,256]{1,0:T(8,128)}, f32[256,256]{1,0:T(8,128)}, f32[1,1,2,2048]{3,2,1,0:T(2,128)}, f32[2]{0:T(128)}, f32[2]{0:T(128)}) custom-call(f32[256,256]{1,0:T(8,128)} %get-tuple-element.9.image, f32[256,256]{1,0:T(8,128)} %get-tuple-element.10.mask, f32[1,1,2,2048]{3,2,1,0:T(2,128)} %get-tuple-element.11.errors, ...), custom_call_target="tpu_custom_call" | custom-call | tf_op jit(solution)/shard_map/deliver_kernel/pallas_call | solution.py:442
